TPU v7x, 32 devices: a whole 2x2x4 slice. The times are simulated.
32 devices in a mesh: dp: 2 (over x), b: 4 (over z), cp: 4 (over y, core).
Axes of the slice: x: 2, y: 2, z: 4, core: 2. Of those that a mesh axis runs over, the one named last changes fastest.
Arguments:
- x: bfloat16 [8, 4096, 2048], P(('dp', 'b'), 'cp'), parts along dimension 0
- ids: int32 [8, 4096, 6], P(('dp', 'b'), 'cp'), parts along dimension 0
- g_attn: bfloat16 [2048], replicated
- w_q: bfloat16 [2048, 3072], replicated
- w_dkv: bfloat16 [2048, 512], replicated
- w_kr: bfloat16 [2048, 64], replicated
- w_uk: bfloat16 [16, 128, 512], replicated
- w_uv: bfloat16 [16, 512, 128], replicated
- w_o: bfloat16 [2048, 2048], replicated
- g_ffn: bfloat16 [2048], replicated
- w_fg: bfloat16 [2048, 10944], replicated
- w_fu: bfloat16 [2048, 10944], replicated
- w_fd: bfloat16 [10944, 2048], replicated
- g_moe: bfloat16 [2048], replicated
- w_r: bfloat16 [2048, 96], replicated
- w_eg: bfloat16 [64, 2048, 1408], P(('b', 'cp'))
- w_eu: bfloat16 [64, 2048, 1408], P(('b', 'cp'))
- w_ed: bfloat16 [64, 1408, 2048], P(('b', 'cp'))
Outputs:
- output: bfloat16 [8, 4096, 2048], P(('dp', 'b'), 'cp'), parts along dimension 0
There are 2 independent parts. A program takes and returns all parts, laid end to end along the dimension named above; an argument that names none is the same for every part.
All inputs are finite; a program needn't handle non-finite values.
Results may differ from a plain program's by a relative error of at most 0.0088785.
Values are sent between devices in bfloat16 or wider.
A program may use at most 1 GiB of HBM per device.

v0:
```python
import jax
import jax.numpy as jnp
from jax import lax
from jax.sharding import PartitionSpec as P

NOPE = 128
ROPE = 64
EPS = 1e-6
SCALE = (NOPE + ROPE) ** -0.5
F32 = jnp.float32
BF16 = jnp.bfloat16


def _rms(v, g):
    vf = v.astype(F32)
    return (vf * lax.rsqrt(jnp.mean(vf * vf, axis=-1, keepdims=True) + EPS) * g.astype(F32)).astype(BF16)


def _rope(v, cos, sin):
    half = ROPE // 2
    v1 = v[..., :half]
    v2 = v[..., half:]
    return jnp.concatenate([v1 * cos - v2 * sin, v1 * sin + v2 * cos], axis=-1)


def _swiglu(z, wg, wu, wd):
    hid = jax.nn.silu(jnp.dot(z, wg, preferred_element_type=F32)) * jnp.dot(z, wu, preferred_element_type=F32)
    return jnp.dot(hid.astype(BF16), wd, preferred_element_type=F32).astype(BF16)


def _prep(x, pos, g_attn, w_q, w_dkv, w_kr, w_uk):
    rows, seq, _ = x.shape
    heads = w_uk.shape[0]
    half = ROPE // 2
    ang = pos.astype(F32)[:, None] * (10000.0 ** (-jnp.arange(half, dtype=F32) / half))[None, :]
    cos = jnp.cos(ang)
    sin = jnp.sin(ang)
    n = _rms(x, g_attn)
    c = jnp.einsum('bsd,dr->bsr', n, w_dkv, preferred_element_type=F32).astype(BF16)
    kr = _rope(jnp.einsum('bsd,de->bse', n, w_kr, preferred_element_type=F32), cos, sin).astype(BF16)
    q = jnp.einsum('bsd,dk->bsk', n, w_q, preferred_element_type=F32).reshape(rows, seq, heads, NOPE + ROPE)
    qt = jnp.einsum('bshn,hnr->bhsr', q[..., :NOPE].astype(BF16), w_uk, preferred_element_type=F32).astype(BF16)
    qr = _rope(jnp.transpose(q[..., NOPE:], (0, 2, 1, 3)), cos, sin).astype(BF16)
    return jnp.concatenate([qt, qr], axis=-1), jnp.concatenate([c, kr], axis=-1)


def _update(state, qc, kv, mask):
    mx, den, acc = state
    r = acc.shape[-1]
    sc = jnp.einsum('bhqe,bke->bhqk', qc, kv, preferred_element_type=F32) * SCALE
    if mask is not None:
        sc = jnp.where(mask, sc, -jnp.inf)
    new = jnp.maximum(mx, jnp.max(sc, axis=-1))
    corr = jnp.exp(mx - new)
    p = jnp.exp(sc - new[..., None])
    den = den * corr + jnp.sum(p, axis=-1)
    pv = jnp.einsum('bhqk,bkr->bhqr', p.astype(BF16), kv[..., :r], preferred_element_type=F32)
    acc = acc * corr[..., None] + pv
    return new, den, acc


def _finish(state, w_uv, w_o):
    _, den, acc = state
    heads, r, vd = w_uv.shape
    lat = (acc / den[..., None]).astype(BF16)
    o = jnp.einsum('bhqr,hrv->bhqv', lat, w_uv, preferred_element_type=F32).astype(BF16)
    return jnp.einsum('cirw,iwe->cre', o, w_o.reshape(heads, vd, -1), preferred_element_type=F32).astype(BF16)


def _gates(u, ids, w_r):
    g = jax.nn.softmax(jnp.dot(u, w_r, preferred_element_type=F32), axis=-1)
    hit = ids[:, :, None] == jnp.arange(g.shape[1], dtype=ids.dtype)
    sel = jnp.sum(jnp.where(hit, g[:, None, :], 0.0), axis=2)
    return sel / jnp.sum(sel, axis=1, keepdims=True)


def _route(lab, gate, ne, cap):
    t = lab.shape[0]
    oh = lab[:, :, None] == jnp.arange(ne, dtype=lab.dtype)
    hit = jnp.any(oh, axis=1)
    ge = jnp.sum(jnp.where(oh, gate[:, :, None], 0.0), axis=1)
    k = jnp.arange(t)
    tri = (k[:, None] > k[None, :]).astype(BF16)
    pre = jnp.dot(tri, hit.astype(BF16), preferred_element_type=F32).astype(lab.dtype)
    sel = hit[:, :, None] & (pre[:, :, None] == jnp.arange(cap, dtype=lab.dtype))
    return sel, jnp.where(sel, ge[:, :, None], 0.0)


def _dispatch(u, sel):
    a = sel.reshape(sel.shape[0], -1).astype(BF16)
    return jnp.einsum('tp,td->pd', a, u, preferred_element_type=F32).astype(BF16)


def _experts(xs, w_eg, w_eu, w_ed):
    hid = (jax.nn.silu(jnp.einsum('gecd,edf->egcf', xs, w_eg, preferred_element_type=F32))
           * jnp.einsum('gecd,edf->egcf', xs, w_eu, preferred_element_type=F32))
    return jnp.einsum('egcf,efd->gecd', hid.astype(BF16), w_ed, preferred_element_type=F32).astype(BF16)


def _combine(ret, u, ids, gate, w, ne):
    zero = jnp.sum(jnp.where(ids >= ne, gate, 0.0), axis=1)
    hi = w.astype(BF16)
    r1 = w - hi.astype(F32)
    mid = r1.astype(BF16)
    lo = (r1 - mid.astype(F32)).astype(BF16)
    part = jnp.einsum('xtp,pd->xtd', jnp.stack([hi, mid, lo]), ret, preferred_element_type=F32)
    return zero[:, None] * u.astype(F32) + jnp.sum(part, axis=0)


def solution(mesh):
    ncp = mesh.shape['cp']
    ngroup = mesh.shape['b'] * ncp
    axes = ('b', 'cp')
    tok = P(('dp', 'b'), 'cp', None)
    rep = P()
    espec = P(('b', 'cp'), None, None)

    def body(x, ids, g_attn, w_q, w_dkv, w_kr, w_uk, w_uv, w_o, g_ffn, w_fg, w_fu, w_fd, g_moe, w_r, w_eg, w_eu, w_ed):
        rows, seq, d = x.shape
        heads, r, _ = w_uv.shape
        top = ids.shape[-1]
        t = rows * seq
        epd = w_eg.shape[0]
        ne = epd * ngroup
        hot = (w_r.shape[1] // top) // 2
        cap = (t + hot - 1) // hot
        i = lax.axis_index('cp')
        loc = jnp.arange(seq)
        qc, kv = _prep(x, i * seq + loc, g_attn, w_q, w_dkv, w_kr, w_uk)
        state = (jnp.full((rows, heads, seq), -jnp.inf, F32), jnp.zeros((rows, heads, seq), F32), jnp.zeros((rows, heads, seq, r), F32))
        state = _update(state, qc, kv, (loc[:, None] >= loc[None, :])[None, None])
        perm = [(k, (k + 1) % ncp) for k in range(ncp)]
        cur = kv
        for step in range(1, ncp):
            cur = lax.ppermute(cur, 'cp', perm)
            state = lax.cond((i - step) % ncp < i,
                             lambda st, kb: _update(st, qc, kb, None),
                             lambda st, kb: st, state, cur)
        a = _finish(state, w_uv, w_o)
        y = (x.astype(F32) + a.astype(F32)).astype(BF16).reshape(t, d)
        f = _swiglu(_rms(y, g_ffn), w_fg, w_fu, w_fd)
        u = _rms(x, g_moe).reshape(t, d)
        idf = ids.reshape(t, top)
        gate = _gates(u, idf, w_r)
        sel, w = _route(idf, gate, ne, cap)
        send = _dispatch(u, sel).reshape(ngroup, epd * cap, d)
        recv = lax.all_to_all(send, axes, 0, 0)
        out = _experts(recv.reshape(ngroup, epd, cap, d), w_eg, w_eu, w_ed)
        ret = lax.all_to_all(out, axes, 0, 0).reshape(ne * cap, d)
        m = _combine(ret, u, idf, gate, w.reshape(t, -1), ne)
        h = y.astype(F32) + f.astype(F32) + m
        return h.astype(BF16).reshape(rows, seq, d)

    return jax.shard_map(body, mesh=mesh, in_specs=(tok, tok) + (rep,) * 13 + (espec,) * 3, out_specs=tok, check_vma=False)
```

profile of v0, /device:TPU:15, one launch (start us, length us, event | category | flops | bytes accessed | tf_op | source)
XLA Modules:
  0.0 2060.9 jit_solution(1467997814449592229)
XLA Ops:
  6.6 20.7 %fusion.54 = pred[1024,64,128]{2,1,0:T(32,128)(4,1)} fusion(s32[1024,64]{1,0:T(8,128)S(1)} %copy.96, pred[1024,64]{1,0:T(8,128)(4,1)S(1)} %copy.95), kind=kLoop, calls=%fused_computation.75 | loop fusion | flops 16777216 | bytes 8716288 | tf_op jit(solution)/shard_map/and | solution.py:85
  27.3 43.6 %fusion.59 = bf16[8192,2048]{1,0:T(8,128)(2,1)} fusion(pred[128,8,64,128]{3,2,1,0:T(32,128)(4,1)} %bitcast.251, bf16[1,1024,2048]{2,1,0:T(8,128)(2,1)} %param.24, f32[2048]{0:T(1024)S(1)} %convert_element_type.247, f32[1024]{0:T(1024)S(1)} %add_rsqrt_fusion.1), kind=kOutput, calls=%fused_computation.81 | convolution fusion | flops 34384904192 | bytes 46149632 | tf_op jit(solution)/shard_map/tp,td->pd/dot_general | solution.py:91
  90.7 710.0 %all-to-all-done = bf16[16,512,2048]{2,1,0:T(8,128)(2,1)} async-done(((bf16[16,512,2048]{2,1,0:T(8,128)(2,1)}), bf16[16,512,2048]{2,1,0:T(8,128)(2,1)}, u32[]{:S(2)}, u32[]{:S(2)}) %all-to-all-start) | async-done | bytes 33554464 | tf_op jit(solution)/shard_map/all_to_all | solution.py:147
  800.7 62.2 %fusion.63 = f32[4,16,128,1408]{3,2,1,0:T(8,128)} fusion(bf16[16,4,128,2048]{3,2,1,0:T(8,128)(2,1)} %bitcast.62, bf16[4,2048,1408]{2,1,0:T(8,128)(2,1)} %param.39), kind=kOutput, calls=%fused_computation.83 | convolution fusion | flops 47244640256 | bytes 102760448 | tf_op jit(solution)/shard_map/gecd,edf->egcf/dot_general | solution.py:95
  862.9 65.7 %multiply_convert_fusion = bf16[4,16,128,1408]{3,2,1,0:T(8,128)(2,1)} fusion(f32[4,16,128,1408]{3,2,1,0:T(8,128)} %fusion.63, bf16[16,4,128,2048]{3,2,1,0:T(8,128)(2,1)} %bitcast.62, bf16[4,2048,1408]{2,1,0:T(8,128)(2,1)} %param.40), kind=kOutput, calls=%fused_computation.63 | convolution fusion | flops 47313846272 | bytes 125829120 | tf_op jit(solution)/shard_map/gecd,edf->egcf/dot_general | solution.py:96
  928.6 60.6 %convert_bitcast_fusion = bf16[16,4,128,2048]{3,2,0,1:T(8,128)(2,1)} fusion(bf16[4,16,128,1408]{3,2,1,0:T(8,128)(2,1)} %multiply_convert_fusion, bf16[4,1408,2048]{2,1,0:T(8,128)(2,1)} %param.41), kind=kOutput, calls=%fused_computation.66 | convolution fusion | flops 47261417472 | bytes 79691776 | tf_op jit(solution)/shard_map/egcf,efd->gecd/dot_general | solution.py:97
  989.2 22.9 %copy.100 = bf16[16,4,128,2048]{3,2,1,0:T(8,128)(2,1)} copy(bf16[16,4,128,2048]{3,2,0,1:T(8,128)(2,1)} %convert_bitcast_fusion) | data formatting | bytes 67108864 | tf_op jit(solution)/shard_map/convert_element_type | solution.py:97
  1023.9 21.5 %broadcast_in_dim.74 = f32[1024,64,128]{2,1,0:T(8,128)} broadcast(f32[1024,64]{1,0:T(8,128)S(1)} %copy.97), dimensions={0,1} | broadcast | bytes 33816576 | tf_op jit(solution)/shard_map/jit(_where)/broadcast_in_dim | solution.py:86
  1045.4 35.9 %broadcast_in_dim.75 = f32[1,1024,8192]{2,1,0:T(8,128)} reshape(f32[1024,64,128]{2,1,0:T(8,128)} %broadcast_in_dim.74) | data formatting | bytes 67108864 | tf_op jit(solution)/shard_map/jit(_where)/broadcast_in_dim | solution.py:86
  1093.3 22.9 %and.56 = pred[1,1024,8192]{2,1,0:T(8,128)(4,1)} reshape(pred[1024,64,128]{2,1,0:T(8,128)(4,1)} %and.55) | data formatting | bytes 16777216 | tf_op jit(solution)/shard_map/and | solution.py:85
  1128.0 35.9 %eq.84 = s32[1,1024,8192]{2,1,0:T(8,128)} reshape(s32[1024,64,128]{2,1,0:T(8,128)} %eq.83) | data formatting | bytes 67108864 | tf_op jit(solution)/shard_map/eq | solution.py:85
  1217.2 35.4 %fusion.40 = (f32[16,1024]{1,0:T(8,128)S(1)}, f32[16,1024,1024]{1,2,0:T(8,128)}) fusion(pred[1024,1024]{0,1:T(8,128)(4,1)S(1)} %iota_compare_fusion.2, bf16[1,1024,32]{1,2,0:T(8,128)(2,1)S(1)} %copy-done.16, bf16[1,1024,32]{1,2,0:T(8,128)(2,1)S(1)} %copy-done.14, bf16[1,1024,512]{1,2,0:T(8,128)(2,1)} %bitcast.256, ...), kind=kOutput, calls=%fused_computation.54 | convolution fusion | flops 19437830144 | bytes 88276992 | tf_op jit(solution)/shard_map/bhqe,bke->bhqk/dot_general | solution.py:50
  1252.6 40.5 %fusion.144 = (bf16[1,1024,8192]{2,1,0:T(8,128)(2,1)}, f32[1,1024,8192]{2,1,0:T(8,128)}) fusion(f32[1,1024,8192]{2,1,0:T(8,128)} %broadcast_in_dim.75, pred[1,1024,8192]{2,1,0:T(8,128)(4,1)} %and.56, s32[1,1024,8192]{2,1,0:T(8,128)} %eq.84, s32[8192]{0:T(1024)S(1)} %iota_bitcast_fusion), kind=kLoop, calls=%fused_computation.175 | loop fusion | flops 33554432 | bytes 125861888 | tf_op jit(solution)/shard_map/convert_element_type | solution.py:102
  1293.1 42.8 %add_bitcast_fusion = f32[1,16,1024,512]{3,2,1,0:T(8,128)} fusion(f32[16,1024]{1,0:T(8,128)S(1)} %exponential_multiply_fusion, f32[16,1024,1024]{1,2,0:T(8,128)} %get-tuple-element.171, f32[16,1024]{1,0:T(8,128)S(1)} %get-tuple-element.170, pred[1024,1024]{0,1:T(8,128)(4,1)S(1)} %iota_compare_fusion.2, bf16[1024,512]{0,1:T(8,128)(2,1)S(1)} %copy-done.10), kind=kOutput, calls=%fused_computation.71 | convolution fusion | flops 17255366656 | bytes 102891520 | tf_op jit(solution)/shard_map/bhqk,bkr->bhqr/dot_general | solution.py:57
  1335.9 21.6 %fusion.42 = f32[16,1024]{1,0:T(8,128)S(1)} fusion(f32[16,1024,1024]{1,2,0:T(8,128)} %get-tuple-element.171, f32[16,1024]{1,0:T(8,128)S(1)} %get-tuple-element.170, pred[1024,1024]{0,1:T(8,128)(4,1)S(1)} %iota_compare_fusion.2), kind=kLoop, calls=%fused_computation.56 | loop fusion | flops 67092480 | bytes 68288512 | tf_op jit(solution)/shard_map/reduce_sum | solution.py:56
  1357.6 35.1 %fusion.65 = (bf16[1,1024,8192]{2,1,0:T(8,128)(2,1)}, bf16[1,1024,8192]{2,1,0:T(8,128)(2,1)}) fusion(f32[1,1024,8192]{2,1,0:T(8,128)} %get-tuple-element.151), kind=kLoop, calls=%fused_computation.85 | loop fusion | flops 58720256 | bytes 67108864 | tf_op jit(solution)/shard_map/convert_element_type | solution.py:104
  1414.4 104.1 %conditional.3 = ((f32[1,16,1024]{2,1,0:T(8,128)S(1)}, f32[1,16,1024]{2,1,0:T(8,128)S(1)}, f32[1,16,1024,512]{3,2,1,0:T(8,128)})) conditional(s32[]{:T(128)} %convert_element_type.223, (f32[1,16,1024]{2,1,0:T(8,128)S(1)}, f32[1,16,1024]{2,1,0:T(8,128)S(1)}, f32[1,16,1024,512]{3,2,1,0:T(8,128)}) %tuple.73, (bf16[1,16,1024,576]{2,3,1,0:T(8,128)(2,1)}, ...), branch_computations={%region_3.4_spmd, %region_4.7_spmd} | conditional | flops 36658266112 | bytes 292945952 | solution.py:136
  1414.4 36.6 %multiply_reduce_fusion = (f32[16,1024]{1,0:T(8,128)S(1)}, f32[16,1024,1024]{1,2,0:T(8,128)}) fusion(bf16[1,16,1024,576]{2,3,1,0:T(8,128)(2,1)} %get-tuple-element.52, bf16[1,1024,576]{1,2,0:T(8,128)(2,1)} %get-tuple-element.128), kind=kOutput, calls=%fused_computation.1 | convolution fusion | flops 19360890880 | bytes 87228416 | tf_op jit(solution)/shard_map/cond/branch_1_fun/bhqe,bke->bhqk/dot_general | solution.py:50
  1451.0 21.4 %fusion.1 = f32[16,1024]{1,0:T(8,128)S(1)} fusion(f32[16,1024,1024]{1,2,0:T(8,128)} %get-tuple-element.157, f32[16,1024]{1,0:T(8,128)S(1)} %bitcast.257), kind=kLoop, calls=%fused_computation.3 | loop fusion | flops 50315264 | bytes 67239936 | tf_op jit(solution)/shard_map/cond/branch_1_fun/reduce_sum | solution.py:56
  1474.1 44.0 %bitcast_add_fusion = f32[1,16,1024,512]{3,2,1,0:T(8,128)} fusion(f32[1,16,1024,512]{3,2,1,0:T(8,128)} %get-tuple-element.55, f32[16,1024]{1,0:T(8,128)S(1)} %get-tuple-element.144, f32[16,1024,1024]{1,2,0:T(8,128)} %get-tuple-element.157, f32[16,1024]{1,0:T(8,128)S(1)} %bitcast.258, bf16[1,1024,576]{2,1,0:T(8,128)(2,1)S(1)} %copy.92), kind=kOutput, calls=%fused_computation.5 | convolution fusion | flops 17246978048 | bytes 135397376 | tf_op jit(solution)/shard_map/cond/branch_1_fun/bhqk,bkr->bhqr/dot_general | solution.py:57
  1518.5 103.8 %conditional.4 = ((f32[1,16,1024]{2,1,0:T(8,128)S(1)}, f32[1,16,1024]{2,1,0:T(8,128)S(1)}, f32[1,16,1024,512]{3,2,1,0:T(8,128)})) conditional(s32[]{:T(128)} %convert_element_type.222, (f32[1,16,1024]{2,1,0:T(8,128)S(1)}, f32[1,16,1024]{2,1,0:T(8,128)S(1)}, f32[1,16,1024,512]{3,2,1,0:T(8,128)}) %get-tuple-element.190, ...), branch_computations={%region_7.8_spmd, %region_8.11_spmd} | conditional | flops 36658266112 | bytes 292945952 | solution.py:136
  1518.5 36.6 %multiply_reduce_fusion.1 = (f32[16,1024]{1,0:T(8,128)S(1)}, f32[16,1024,1024]{1,2,0:T(8,128)}) fusion(bf16[1,16,1024,576]{2,3,1,0:T(8,128)(2,1)} %get-tuple-element.57, bf16[1,1024,576]{1,2,0:T(8,128)(2,1)} %get-tuple-element.133), kind=kOutput, calls=%fused_computation.18 | convolution fusion | flops 19360890880 | bytes 87228416 | tf_op jit(solution)/shard_map/cond/branch_1_fun/bhqe,bke->bhqk/dot_general | solution.py:50
  1555.1 21.4 %fusion.14 = f32[16,1024]{1,0:T(8,128)S(1)} fusion(f32[16,1024,1024]{1,2,0:T(8,128)} %get-tuple-element.159, f32[16,1024]{1,0:T(8,128)S(1)} %bitcast.259), kind=kLoop, calls=%fused_computation.20 | loop fusion | flops 50315264 | bytes 67239936 | tf_op jit(solution)/shard_map/cond/branch_1_fun/reduce_sum | solution.py:56
  1578.3 44.0 %bitcast_add_fusion.2 = f32[1,16,1024,512]{3,2,1,0:T(8,128)} fusion(f32[1,16,1024,512]{3,2,1,0:T(8,128)} %get-tuple-element.60, f32[16,1024]{1,0:T(8,128)S(1)} %get-tuple-element.146, f32[16,1024,1024]{1,2,0:T(8,128)} %get-tuple-element.159, f32[16,1024]{1,0:T(8,128)S(1)} %bitcast.260, bf16[1,1024,576]{2,1,0:T(8,128)(2,1)S(1)} %copy.93), kind=kOutput, calls=%fused_computation.22 | convolution fusion | flops 17246978048 | bytes 135397376 | tf_op jit(solution)/shard_map/cond/branch_1_fun/bhqk,bkr->bhqr/dot_general | solution.py:57
  1622.3 104.1 %conditional.5 = ((f32[1,16,1024]{2,1,0:T(8,128)S(1)}, f32[1,16,1024,512]{3,2,1,0:T(8,128)})) conditional(s32[]{:T(128)} %convert_element_type.221, (f32[1,16,1024]{2,1,0:T(8,128)S(1)}, f32[1,16,1024,512]{3,2,1,0:T(8,128)}) %tuple.28, (bf16[1,16,1024,576]{2,3,1,0:T(8,128)(2,1)}, bf16[1,1024,576]{1,2,0:T(8,128)(2,1)}, ...), branch_computations={%region_11.12_spmd, %region_12.15_spmd} | conditional | flops 36658282496 | bytes 292814848 | solution.py:136
  1622.4 36.6 %multiply_reduce_fusion.2 = (f32[16,1024]{1,0:T(8,128)S(1)}, f32[16,1024,1024]{1,2,0:T(8,128)}) fusion(bf16[1,16,1024,576]{2,3,1,0:T(8,128)(2,1)} %get-tuple-element.63, bf16[1,1024,576]{1,2,0:T(8,128)(2,1)} %get-tuple-element.138), kind=kOutput, calls=%fused_computation.35 | convolution fusion | flops 19360890880 | bytes 87228416 | tf_op jit(solution)/shard_map/cond/branch_1_fun/bhqe,bke->bhqk/dot_general | solution.py:50
  1659.0 21.4 %fusion.27 = f32[16,1024]{1,0:T(8,128)S(1)} fusion(f32[16,1024,1024]{1,2,0:T(8,128)} %get-tuple-element.155, f32[16,1024]{1,0:T(8,128)S(1)} %get-tuple-element.153), kind=kLoop, calls=%fused_computation.37 | loop fusion | flops 50315264 | bytes 67239936 | tf_op jit(solution)/shard_map/cond/branch_1_fun/reduce_sum | solution.py:56
  1682.2 44.0 %bitcast_add_fusion.4 = f32[1,16,1024,512]{3,2,1,0:T(8,128)} fusion(f32[1,16,1024,512]{3,2,1,0:T(8,128)} %get-tuple-element.65, f32[16,1024]{1,0:T(8,128)S(1)} %get-tuple-element.152, f32[16,1024,1024]{1,2,0:T(8,128)} %get-tuple-element.155, f32[16,1024]{1,0:T(8,128)S(1)} %get-tuple-element.153, bf16[1,1024,576]{2,1,0:T(8,128)(2,1)S(1)} %copy.94), kind=kOutput, calls=%fused_computation.39 | convolution fusion | flops 17246978048 | bytes 135397376 | tf_op jit(solution)/shard_map/cond/branch_1_fun/bhqk,bkr->bhqr/dot_general | solution.py:57
  1757.1 54.5 %fusion.117 = f32[1024,10944]{0,1:T(8,128)} fusion(bf16[2048,10944]{0,1:T(8,128)(2,1)} %param.34, bf16[1024,2048]{1,0:T(8,128)(2,1)S(1)} %get-tuple-element.173, f32[2048]{0:T(1024)S(1)} %copy-done.23, f32[1024]{0:T(1024)S(1)} %add_rsqrt_fusion), kind=kOutput, calls=%fused_computation.140 | convolution fusion | flops 45910851584 | bytes 93859840 | tf_op jit(solution)/shard_map/dot_general | solution.py:27
  1811.6 65.3 %multiply_convert_fusion.1 = bf16[1024,10944]{0,1:T(8,128)(2,1)} fusion(f32[1024,10944]{0,1:T(8,128)} %fusion.117, bf16[2048,10944]{0,1:T(8,128)(2,1)} %param.35, bf16[1024,2048]{1,0:T(8,128)(2,1)} %copy-done.36, f32[2048]{0:T(1024)S(1)} %copy-done.23, f32[1024]{0:T(1024)S(1)} %add_rsqrt_fusion), kind=kOutput, calls=%fused_computation.64 | convolution fusion | flops 45978091520 | bytes 116273152 | tf_op jit(solution)/shard_map/dot_general | solution.py:27
  1877.0 122.8 %fusion.89 = f32[1024,2048]{1,0:T(8,128)} fusion(bf16[8192,2048,1]{1,0,2:T(8,128)(2,1)} %bitcast.71, bf16[1,1024,8192]{2,1,0:T(8,128)(2,1)} %get-tuple-element.161, bf16[1,1024,8192]{2,1,0:T(8,128)(2,1)} %get-tuple-element.160, bf16[1,1024,8192]{2,1,0:T(8,128)(2,1)} %get-tuple-element.150), kind=kOutput, calls=%fused_computation.115 | convolution fusion | flops 103133741056 | bytes 92274688 | tf_op jit(solution)/shard_map/xtp,pd->xtd/dot_general | solution.py:106
  1999.8 60.9 %fusion.94 = bf16[1,1024,2048]{2,1,0:T(8,128)(2,1)} fusion(f32[1024,2048]{1,0:T(8,128)} %fusion.89, bf16[1024,2048]{1,0:T(8,128)(2,1)} %copy-done.36, f32[1024]{0:T(1024)S(1)} %copy-done.28, bf16[1024,10944]{0,1:T(8,128)(2,1)} %multiply_convert_fusion.1, bf16[10944,2048]{1,0:T(8,128)(2,1)} %param.36, f32[2048]{0:T(1024)S(1)} %copy-done.22, ...), kind=kOutput, calls=%fused_computation.118 | convolution fusion | flops 45929725952 | bytes 88227840 | tf_op jit(solution)/shard_map/dot_general | solution.py:28
  (133 shorter events, 172.6 us)
Async XLA Ops:
  0.0 1205.5 %copy-start = (bf16[16,128,512]{2,1,0:T(8,128)(2,1)S(1)}, bf16[16,128,512]{2,1,0:T(8,128)(2,1)}, u32[]{:S(2)}) copy-start(bf16[16,128,512]{2,1,0:T(8,128)(2,1)} %param.30) | copy-start | bytes 6291460
  2.6 68.3 %copy-start.7 = (pred[1024,64]{1,0:T(8,128)(4,1)}, pred[1024,64]{1,0:T(8,128)(4,1)S(1)}, u32[]{:S(2)}) copy-start(pred[1024,64]{1,0:T(8,128)(4,1)S(1)} %copy.95) | copy-start | bytes 196612
  2.8 68.1 %copy-start.3 = (s32[1024,64]{1,0:T(8,128)}, s32[1024,64]{1,0:T(8,128)S(1)}, u32[]{:S(2)}) copy-start(s32[1024,64]{1,0:T(8,128)S(1)} %copy.96) | copy-start | bytes 786436
  3.5 67.4 %copy-start.20 = (f32[2048]{0:T(1024)}, f32[2048]{0:T(1024)S(1)}, u32[]{:S(2)}) copy-start(f32[2048]{0:T(1024)S(1)} %convert_element_type.247) | copy-start | bytes 24580
  6.6 75.9 %copy-start.29 = (f32[1024]{0:T(1024)}, f32[1024]{0:T(1024)S(1)}, u32[]{:S(2)}) copy-start(f32[1024]{0:T(1024)S(1)} %add_rsqrt_fusion.1) | copy-start | bytes 12292
  70.9 729.8 %all-to-all-start = ((bf16[16,512,2048]{2,1,0:T(8,128)(2,1)}), bf16[16,512,2048]{2,1,0:T(8,128)(2,1)}, u32[]{:S(2)}, u32[]{:S(2)}) async-start(bf16[16,512,2048]{2,1,0:T(8,128)(2,1)} %bitcast.249), calls=%async_computation | async-start | bytes 67108864 | tf_op jit(solution)/shard_map/all_to_all | solution.py:147
  78.2 9.7 copy-start.24
  78.3 9.7 copy-start.32
  82.5 7.6 copy-start.13
  82.6 7.6 copy-start.15
  90.1 1267.3 %collective-permute-start = (bf16[1,1024,576]{1,2,0:T(8,128)(2,1)}, bf16[1,1024,576]{1,2,0:T(8,128)(2,1)}, u32[]{:S(2)}, u32[]{:S(2)}) collective-permute-start(bf16[1,1024,576]{1,2,0:T(8,128)(2,1)} %pad_maximum_fusion.1), channel_id=1, source_target_pairs={{0,1},{1,2},{2,3},{3,0},{4,5},{5,6},{6,7},{7,4},{8,9},{9,10},{10,1... | collective-permute-start | bytes 3538952 | tf_op jit(solution)/shard_map/ppermute | solution.py:135
  1012.2 10.3 copy-start.12
  1012.2 10.7 copy-start.17
  1012.2 864.8 %all-to-all-start.1 = ((bf16[16,4,128,2048]{3,2,1,0:T(8,128)(2,1)}), bf16[16,4,128,2048]{3,2,1,0:T(8,128)(2,1)}, u32[]{:S(2)}, u32[]{:S(2)}) async-start(bf16[16,4,128,2048]{3,2,1,0:T(8,128)(2,1)} %copy.100), calls=%async_computation.1 | async-start | bytes 67108864 | tf_op jit(solution)/shard_map/all_to_all | solution.py:149
  1045.4 35.9 %copy-start.8 = (pred[1024,64]{1,0:T(8,128)(4,1)S(1)}, pred[1024,64]{1,0:T(8,128)(4,1)}, u32[]{:S(2)}) copy-start(pred[1024,64]{1,0:T(8,128)(4,1)} %copy-done.7) | copy-start | bytes 196612
  1081.3 34.8 %copy-start.4 = (s32[1024,64]{1,0:T(8,128)S(1)}, s32[1024,64]{1,0:T(8,128)}, u32[]{:S(2)}) copy-start(s32[1024,64]{1,0:T(8,128)} %copy-done.3) | copy-start | bytes 786436
  1163.9 16.6 copy-start.19
  1163.9 16.7 copy-start.33
  1163.9 17.2 copy-start.25
  1205.5 11.7 copy-start.14
  1205.5 11.7 copy-start.16
  1252.6 40.5 %copy-start.10 = (bf16[1024,512]{0,1:T(8,128)(2,1)S(1)}, bf16[1024,512]{0,1:T(8,128)(2,1)}, u32[]{:S(2)}) copy-start(bf16[1024,512]{0,1:T(8,128)(2,1)} %copy-done.9) | copy-start | bytes 3145732
  1357.5 35.9 %collective-permute-start.1 = (bf16[1,1024,576]{1,2,0:T(8,128)(2,1)}, bf16[1,1024,576]{1,2,0:T(8,128)(2,1)}, u32[]{:S(2)}, u32[]{:S(2)}) collective-permute-start(bf16[1,1024,576]{1,2,0:T(8,128)(2,1)} %collective-permute-done), channel_id=1, source_target_pairs={{0,1},{1,2},{2,3},{3,0},{4,5},{5,6},{6,7},{7,4},{8,9},{9,10},{10,1... | collective-permute-start | bytes 3538952 | tf_op jit(solution)/shard_map/ppermute | solution.py:135
  1357.5 35.2 %copy-start.27 = (bf16[2048]{0:T(1024)(128)(2,1)S(1)}, bf16[2048]{0:T(1024)(128)(2,1)}, u32[]{:S(2)}) copy-start(bf16[2048]{0:T(1024)(128)(2,1)} %param.33) | copy-start | bytes 12292
  1357.5 38.3 %copy-start.5 = (bf16[1,16,1024,32]{2,3,1,0:T(8,128)(2,1)S(1)}, bf16[1,16,1024,32]{2,3,1,0:T(8,128)(2,1)}, u32[]{:S(2)}) copy-start(bf16[1,16,1024,32]{2,3,1,0:T(8,128)(2,1)} %get-tuple-element.162) | copy-start | bytes 3145732
  1357.6 38.3 %copy-start.6 = (bf16[1,16,1024,32]{2,3,1,0:T(8,128)(2,1)S(1)}, bf16[1,16,1024,32]{2,3,1,0:T(8,128)(2,1)}, u32[]{:S(2)}) copy-start(bf16[1,16,1024,32]{2,3,1,0:T(8,128)(2,1)} %get-tuple-element.163) | copy-start | bytes 3145732
  1393.3 228.9 %collective-permute-start.2 = (bf16[1,1024,576]{1,2,0:T(8,128)(2,1)}, bf16[1,1024,576]{1,2,0:T(8,128)(2,1)}, u32[]{:S(2)}, u32[]{:S(2)}) collective-permute-start(bf16[1,1024,576]{1,2,0:T(8,128)(2,1)} %collective-permute-done.1), channel_id=1, source_target_pairs={{0,1},{1,2},{2,3},{3,0},{4,5},{5,6},{6,7},{7,4},{8,9},{9,10},{10,1... | collective-permute-start | bytes 3538952 | tf_op jit(solution)/shard_map/ppermute | solution.py:135
  1742.1 15.0 copy-start.23
  1877.0 122.8 %copy-start.22 = (f32[2048]{0:T(1024)S(1)}, f32[2048]{0:T(1024)}, u32[]{:S(2)}) copy-start(f32[2048]{0:T(1024)} %copy-done.20) | copy-start | bytes 24580
  1877.0 122.8 %copy-start.28 = (f32[1024]{0:T(1024)S(1)}, f32[1024]{0:T(1024)}, u32[]{:S(2)}) copy-start(f32[1024]{0:T(1024)} %get-tuple-element.148) | copy-start | bytes 12292
  1877.0 122.8 %copy-start.31 = (f32[1024]{0:T(1024)S(1)}, f32[1024]{0:T(1024)}, u32[]{:S(2)}) copy-start(f32[1024]{0:T(1024)} %copy-done.29) | copy-start | bytes 12292
  1999.8 60.9 %copy-start.1 = (bf16[16,128,512]{2,1,0:T(8,128)(2,1)S(1)}, bf16[16,128,512]{2,1,0:T(8,128)(2,1)}, u32[]{:S(2)}) copy-start(bf16[16,128,512]{2,1,0:T(8,128)(2,1)} %param.30) | copy-start | bytes 6291460
  (10 other events, 45.7 us)
where the time goes:
time: 2070 us; the launch traced here: 2060 us
  matrix products  927 us (45%)
  waiting for transfers between devices  710 us (34%)
  other arithmetic  211 us (10%)
  local copies, waits for them, and re-layouts  195 us (9%)
    all_to_all x1, waiting for transfers between devices, body(): recv = lax.all_to_all(send, axes, 0, 0)  710 us
    dot_general x4, matrix products, _update(): jnp.einsum('bhqk,bkr->bhqr', p.astype(BF16), kv[..., :r], preferred_eleme...  175 us
    dot_general x4, matrix products, _update(): jnp.einsum('bhqe,bke->bhqk', qc, kv, preferred_element_type=F32) * SCALE  145 us
    dot_general x1, matrix products, _combine(): jnp.einsum('xtp,pd->xtd', jnp.stack([hi, mid, lo]), ret, preferred_elemen...  123 us
    reduce_sum x4, other arithmetic, _update(): den = den * corr + jnp.sum(p, axis=-1)  85.6 us
    dot_general x1, matrix products, _experts(): jnp.einsum('gecd,edf->egcf', xs, w_eu, preferred_element_type=F32)  65.7 us
    dot_general x1, matrix products, _swiglu(): jnp.dot(z, wu, preferred_element_type=F32)  65.3 us
    dot_general x1, matrix products, _experts(): jnp.einsum('gecd,edf->egcf', xs, w_eg, preferred_element_type=F32)  62.2 us
  transfers between devices with their start and end apart: 5, of which 1 were waited for; matrix products, arithmetic and copies ran while one was open for 52% of the time, Pallas kernels for 0%

commit v1 on v0

v1 whole, which is shorter than its diff:
```python
import functools

import jax
import jax.numpy as jnp
from jax import lax
from jax.experimental import pallas as pl
from jax.experimental.pallas import tpu as pltpu
from jax.sharding import PartitionSpec as P


F32 = jnp.float32
BF16 = jnp.bfloat16
EPS = 1e-6


NOPE, ROPE = 128, 64
SCALE=(NOPE+ROPE)**-0.5
LOG2E=1.4426950408889634


def _rope(v, c, sa, sb):
    return v*c + pltpu.roll(v, 32, 1)*sa + pltpu.roll(v, 96, 1)*sb


def _pre_body(x_ref, ga_ref, gm_ref, wc_ref, wk_ref, wr_ref, c_ref, sa_ref, sb_ref, n_ref, kv_ref, lg_ref, *u_refs):
    xf = x_ref[...].astype(F32)
    z = xf * lax.rsqrt(jnp.mean(xf*xf, axis=-1, keepdims=True) + EPS)
    n = (z * ga_ref[...].astype(F32)).astype(BF16)
    u = (z * gm_ref[...].astype(F32)).astype(BF16)
    n_ref[...] = n
    w = u.shape[1]//len(u_refs)
    for k, r in enumerate(u_refs): r[...] = u[:, k*w:(k+1)*w]
    r = wc_ref.shape[1]
    kv_ref[:, :r] = jnp.dot(n, wc_ref[...], preferred_element_type=F32).astype(BF16)
    kr = jnp.dot(n, wk_ref[...], preferred_element_type=F32)
    kr = jnp.concatenate([kr, jnp.zeros_like(kr)], axis=1)
    kv_ref[:, r:] = _rope(kr, c_ref[...], sa_ref[...], sb_ref[...]).astype(BF16)
    lg_ref[...] = jnp.dot(u, wr_ref[...], preferred_element_type=F32)


def pre(x, ga, gm, wc, wk, wr, tabs, nk, tm=256):
    t, d = x.shape
    r = wc.shape[1]
    row = lambda w: pl.BlockSpec((tm, w), lambda i: (i, 0))
    full = lambda a: pl.BlockSpec(a.shape, lambda i: (0,)*a.ndim)
    ns = wr.shape[1]
    return pl.pallas_call(_pre_body, grid=(t//tm,),
        in_specs=[row(d), full(ga), full(gm), full(wc), full(wk), full(wr), row(128), row(128), row(128)],
        out_specs=[row(d), row(r+128), row(ns)] + [row(d//nk)]*nk,
        out_shape=[jax.ShapeDtypeStruct((t, d), BF16), jax.ShapeDtypeStruct((t, r+128), BF16), jax.ShapeDtypeStruct((t, ns), F32)]
                  + [jax.ShapeDtypeStruct((t, d//nk), BF16)]*nk,
        name="pre", cost_estimate=pl.CostEstimate(flops=1024, bytes_accessed=6*t*d, transcendentals=0),
        compiler_params=pltpu.CompilerParams(dimension_semantics=("arbitrary",), vmem_limit_bytes=40<<20))(x, ga, gm, wc, wk, wr, *tabs)


def _qproj_body(n_ref, w_ref, uk_ref, c_ref, sa_ref, sb_ref, o_ref):
    q = jnp.dot(n_ref[...], w_ref[...], preferred_element_type=F32)
    t0, t1, t2 = q[:, :128], q[:, 128:256], q[:, 256:]
    r1, r2 = pltpu.roll(t1, 64, 1), pltpu.roll(t2, 64, 1)
    lane = lax.broadcasted_iota(jnp.int32, t0.shape, 1)
    nope = (t0, jnp.where(lane < 64, r1, r2))
    rope = (t1, r2)
    c, sa, sb = c_ref[...], sa_ref[...], sb_ref[...]
    r = uk_ref.shape[2]
    for k in range(2):
        o_ref[k, :, :r] = jnp.dot(nope[k].astype(BF16), uk_ref[k], preferred_element_type=F32).astype(BF16)
        o_ref[k, :, r:] = _rope(rope[k], c, sa, sb).astype(BF16)


def qproj(n, wq, wuk, tabs, tm=512):
    t, d = n.shape
    h, _, r = wuk.shape
    tab = pl.BlockSpec((tm, 128), lambda j, i: (i, 0))
    return pl.pallas_call(_qproj_body, grid=(h//2, t//tm),
        in_specs=[pl.BlockSpec((tm, d), lambda j, i: (i, 0)), pl.BlockSpec((d, 384), lambda j, i: (0, j)),
                  pl.BlockSpec((2, NOPE, r), lambda j, i: (j, 0, 0)), tab, tab, tab],
        out_specs=pl.BlockSpec((2, tm, r+128), lambda j, i: (j, i, 0)),
        out_shape=jax.ShapeDtypeStruct((h, t, r+128), BF16), name="qproj",
        cost_estimate=pl.CostEstimate(flops=1024, bytes_accessed=2*(h//2*t*d+d*h*192+t*h*(r+128)), transcendentals=0),
        compiler_params=pltpu.CompilerParams(dimension_semantics=("arbitrary","arbitrary"), vmem_limit_bytes=40<<20))(n, wq, wuk, *tabs)


def _attn_body(tq, sub, i_ref, q_ref, k0, k1, k2, k3, uv_ref, o_ref, m_ref, l_ref, acc_ref):
    at = i_ref[0]
    seq, r = q_ref.shape[1], uv_ref.shape[1]
    CF = SCALE*LOG2E
    nt = (((1,), (1,)), ((), ()))
    def block(rows, kv, diag, first):
        q = q_ref[0, rows:rows+sub]
        s = lax.dot_general(q, kv, nt, preferred_element_type=F32)
        if diag is not None:
            rr = lax.broadcasted_iota(jnp.int32, s.shape, 0) + diag
            cc = lax.broadcasted_iota(jnp.int32, s.shape, 1)
            s = jnp.where(rr >= cc, s, -jnp.inf)
        mx = jnp.max(s, axis=1, keepdims=True)
        if first:
            m = jnp.broadcast_to(mx, (sub, 128))
            p = jnp.exp2((s - mx)*CF)
            l_ref[rows:rows+sub] = jnp.broadcast_to(jnp.sum(p, axis=1, keepdims=True), (sub, 128))
            acc_ref[rows:rows+sub] = jnp.dot(p.astype(BF16), kv[:, :r], preferred_element_type=F32)
        else:
            m0 = m_ref[rows:rows+sub]
            m = jnp.maximum(m0, mx)
            corr = jnp.exp2((m0 - m)*CF)
            p = jnp.exp2((s - m[:, :1])*CF)
            l_ref[rows:rows+sub] = l_ref[rows:rows+sub]*corr + jnp.sum(p, axis=1, keepdims=True)
            acc_ref[rows:rows+sub] = acc_ref[rows:rows+sub]*corr[:, :1] + jnp.dot(p.astype(BF16), kv[:, :r], preferred_element_type=F32)
        m_ref[rows:rows+sub] = m
    for t0 in range(0, seq, tq):
        for rows in range(t0, t0+tq, sub):
            block(rows, k0[:t0+tq], rows, True)
    for ok, kr in ((at >= 2, k1), (lax.rem(at, 2) == 1, k2), (at >= 2, k3)):
        @pl.when(ok)
        def _():
            for rows in range(0, seq, sub):
                block(rows, kr[...], None, False)
    for rows in range(0, seq, 256):
        lat = (acc_ref[rows:rows+256] / l_ref[rows:rows+256, :1]).astype(BF16)
        o_ref[rows:rows+256] = jnp.dot(lat, uv_ref[0], preferred_element_type=F32).astype(BF16)


def attn(i, q, kvs, wuv, part, parts, tq=512, sub=512):
    h, t, w = q.shape
    r, vd = wuv.shape[1:]
    hp = h // parts
    o = part * hp
    kspec = pl.BlockSpec((t, w), lambda j, *_: (0, 0), pipeline_mode=pl.Buffered(1))
    return pl.pallas_call(functools.partial(_attn_body, tq, sub),
        grid_spec=pltpu.PrefetchScalarGridSpec(num_scalar_prefetch=1, grid=(hp,),
            in_specs=[pl.BlockSpec((1, t, w), lambda j, *_: (j + o, 0, 0)), kspec, kspec, kspec, kspec,
                      pl.BlockSpec((1, r, vd), lambda j, *_: (j + o, 0, 0))],
            out_specs=pl.BlockSpec((t, vd), lambda j, *_: (0, j)),
            scratch_shapes=[pltpu.VMEM((t, 128), F32), pltpu.VMEM((t, 128), F32), pltpu.VMEM((t, r), F32)]),
        out_shape=jax.ShapeDtypeStruct((t, hp*vd), BF16), name="attn",
        cost_estimate=pl.CostEstimate(flops=1024, bytes_accessed=2*hp*t*w, transcendentals=hp*t*t*5//2),
        compiler_params=pltpu.CompilerParams(dimension_semantics=("arbitrary",), vmem_limit_bytes=60<<20))(i, q, *kvs, wuv)


def _pick_body(h_ref, rank_ref, u_ref, o_ref):
    ne, cap = o_ref.shape[0], o_ref.shape[2]
    t = u_ref.shape[1]
    row = lax.broadcasted_iota(jnp.int32, (cap, t), 0)
    oh = jnp.concatenate([(rank_ref[0, e:e+1, :] == row).astype(F32).astype(BF16) for e in range(ne)], axis=0)
    o = jnp.dot(oh, u_ref[0], preferred_element_type=F32).astype(BF16)
    for e in range(ne):
        o_ref[e, 0] = o[e*cap:(e+1)*cap]


def pick(h, rank, u, nl, cap):
    _, E, t = rank.shape
    d = u.shape[-1]
    return pl.pallas_call(
        _pick_body,
        grid_spec=pltpu.PrefetchScalarGridSpec(num_scalar_prefetch=1, grid=(nl,),
            in_specs=[pl.BlockSpec((1, E, t), lambda s, h: (h[0] + s, 0, 0)), pl.BlockSpec((1, t, d), lambda s, h: (h[1] + s, 0, 0))],
            out_specs=pl.BlockSpec((E, 1, cap, d), lambda s, h: (0, s, 0, 0))),
        out_shape=jax.ShapeDtypeStruct((E, nl, cap, d), BF16), name="pick",
        cost_estimate=pl.CostEstimate(flops=1024, bytes_accessed=2*nl*(t+E*cap)*d, transcendentals=0),
        compiler_params=pltpu.CompilerParams(dimension_semantics=("arbitrary",), vmem_limit_bytes=40<<20))(h, rank, u)


def _expert_body(e0, ne, n_ref, lst_ref, x_hbm, wg_hbm, wu_hbm, wd_hbm, o_hbm,
                 x_ref, w_ref, wd_ref, hid_ref, f_ref, ob_ref, xsem, wsem, dsem, osem):
    _, S, cap, d = x_hbm.shape
    ff = wg_hbm.shape[-1]
    kc = d // 4
    half = S // 2
    tm = half * cap
    def wcopies(e):
        b = e % 2
        out = []
        for i in range(4):
            out.append(pltpu.make_async_copy(wg_hbm.at[e, pl.ds(i*kc, kc)], w_ref.at[b, pl.ds(i*kc, kc), pl.ds(0, ff)], wsem.at[b, 0, i]))
            out.append(pltpu.make_async_copy(wu_hbm.at[e, pl.ds(i*kc, kc)], w_ref.at[b, pl.ds(i*kc, kc), pl.ds(ff, ff)], wsem.at[b, 1, i]))
        return out
    def dcopy(e):
        return pltpu.make_async_copy(wd_hbm.at[e], wd_ref.at[e % 2], dsem.at[e % 2])
    def xcopies(e):
        return [pltpu.make_async_copy(x_hbm.at[e, lst_ref[e*S + j]], x_ref.at[e % 2, pl.ds(j*cap, cap)], xsem.at[e % 2, j]) for j in range(S)]
    def ocopies(e, m):
        out = []
        for j in range(half):
            s = lst_ref[e*S + m*half + j]
            out.append(pltpu.make_async_copy(ob_ref.at[m, pl.ds(j*cap*16, cap*16)], o_hbm.at[pl.ds((s*ne + e - e0)*cap*16, cap*16)], osem.at[m, j]))
        return out
    def when(e, m):
        return n_ref[e] > m*half
    def load(e):
        @pl.when(when(e, 0))
        def _():
            for c in wcopies(e): c.start()
            for c in xcopies(e): c.start()
            dcopy(e).start()
    def out_wait(e, m):
        @pl.when(when(e, m))
        def _():
            for c in ocopies(e, m): c.wait()
    load(e0)
    for e in range(e0, e0 + ne):
        b = e % 2
        if e + 1 < e0 + ne:
            load(e + 1)
        @pl.when(when(e, 0))
        def _():
            for c in xcopies(e): c.wait()
            for c in wcopies(e): c.wait()
        for m in range(2):
            if e > e0:
                out_wait(e - 1, m)
            @pl.when(when(e, m))
            def _():
                gu = jnp.dot(x_ref[b, m*tm:(m+1)*tm], w_ref[b], preferred_element_type=F32)
                g, u = gu[:, :ff], gu[:, ff:]
                hid_ref[...] = (g * jax.nn.sigmoid(g) * u).astype(BF16)
                if m == 0:
                    dcopy(e).wait()
                for c0 in range(0, d, 1024):
                    o = jnp.dot(hid_ref[...], wd_ref[b, :, c0:c0+1024], preferred_element_type=F32)
                    for k in range(0, 1024, 128):
                        f_ref[pl.ds((c0+k)//128, tm, stride=16), :] = o[:, k:k+128]
                ob_ref[m] = f_ref[...].astype(BF16)
                for c in ocopies(e, m): c.start()
    for m in range(2):
        out_wait(e0 + ne - 1, m)


def expert(e0, ne, n, lst, xg, wg, wu, wd):
    E, S, cap, d = xg.shape
    ff = wg.shape[-1]
    tm = S // 2 * cap
    any_ = pl.BlockSpec(memory_space=pl.ANY)
    return pl.pallas_call(
        functools.partial(_expert_body, e0, ne),
        grid_spec=pltpu.PrefetchScalarGridSpec(num_scalar_prefetch=2, grid=(), in_specs=[any_]*4, out_specs=any_,
            scratch_shapes=[pltpu.VMEM((2, S*cap, d), BF16), pltpu.VMEM((2, d, 2*ff), BF16), pltpu.VMEM((2, ff, d), BF16),
                            pltpu.VMEM((tm, ff), BF16), pltpu.VMEM((tm*16, 128), F32), pltpu.VMEM((2, tm*16, 128), BF16),
                            pltpu.SemaphoreType.DMA((2, S)), pltpu.SemaphoreType.DMA((2, 2, 4)), pltpu.SemaphoreType.DMA((2,)),
                            pltpu.SemaphoreType.DMA((2, S//2))]),
        out_shape=jax.ShapeDtypeStruct((S*ne*cap*16, 128), BF16), name="expert",
        cost_estimate=pl.CostEstimate(flops=1024, bytes_accessed=6*E*d*ff+4*E*S*cap*d, transcendentals=E*S*cap*ff),
        compiler_params=pltpu.CompilerParams(vmem_limit_bytes=62<<20))(n, lst, xg, wg, wu, wd)


def _rows(k_ref, idx_ref, w_ref, r_refs, buf, scr, sem, tt):
    n = buf.shape[0] - 16
    m = n // len(r_refs)
    i = pl.program_id(0)
    t = pl.num_programs(0)*tt
    @pl.when(i == 0)
    def _():
        cs = [pltpu.make_async_copy(r, buf.at[pl.ds(c*m, m)], sem.at[c]) for c, r in enumerate(r_refs)]
        for c in cs: c.start()
        buf[n:n+16] = jnp.zeros((16, 128), BF16)
        for c in cs: c.wait()
    def row(j, q):
        g = j*t + i*tt + q
        return w_ref[g]*buf[pl.ds(pl.multiple_of(idx_ref[g]*16, 16), 16), :].astype(F32)
    def first(q, _):
        scr[pl.ds(pl.multiple_of(q*16, 16), 16), :] = row(0, q)
        return 0
    lax.fori_loop(0, tt, first, 0, unroll=8)
    def more(j, _):
        def add(q, _):
            s = pl.ds(pl.multiple_of(q*16, 16), 16)
            scr[s, :] = scr[s, :] + row(j, q)
            return 0
        lax.fori_loop(0, tt, add, 0, unroll=8)
        return 0
    lax.fori_loop(1, k_ref[0], more, 0)


def _part_body(nr, k_ref, idx_ref, w_ref, *rest):
    r_refs, (*prev, o_ref, buf, sem) = rest[:nr], rest[nr:]
    _rows(k_ref, idx_ref, w_ref, r_refs, buf, o_ref, sem, o_ref.shape[0]//16)
    for p in prev:
        o_ref[...] += p[...]


def part(k, idx, w, rets, prev, t, tt=128):
    n = sum(r.shape[0] for r in rets)
    blk = pl.BlockSpec((tt*16, 128), lambda i, *_: (i, 0))
    return pl.pallas_call(functools.partial(_part_body, len(rets)),
        grid_spec=pltpu.PrefetchScalarGridSpec(num_scalar_prefetch=3, grid=(t//tt,),
            in_specs=[pl.BlockSpec(memory_space=pl.ANY)]*len(rets) + [blk]*len(prev), out_specs=blk,
            scratch_shapes=[pltpu.VMEM((n+16, 128), BF16), pltpu.SemaphoreType.DMA((len(rets),))]),
        out_shape=jax.ShapeDtypeStruct((t*16, 128), F32), name="part",
        cost_estimate=pl.CostEstimate(flops=1024, bytes_accessed=2*n*128+12*t*2048, transcendentals=0),
        compiler_params=pltpu.CompilerParams(dimension_semantics=("arbitrary",), vmem_limit_bytes=40<<20))(k, idx, w, *rets, *prev)


def _final_body(nr, k_ref, idx_ref, w_ref, z_ref, y_ref, f_ref, u_ref, *rest):
    r_refs, (*prev, h_ref, buf, scr, sem) = rest[:nr], rest[nr:]
    tt = y_ref.shape[0]
    _rows(k_ref, idx_ref, w_ref, r_refs, buf, scr, sem, tt)
    for p in prev:
        scr[...] += p[...]
    z = z_ref[...]
    for k in range(16):
        c = slice(k*128, (k+1)*128)
        m = scr[pl.ds(k, tt, stride=16), :] + z*u_ref[:, c].astype(F32)
        h_ref[:, c] = (y_ref[:, c].astype(F32) + f_ref[:, c].astype(F32) + m).astype(BF16)


def final(k, idx, w, rets, zero, y, f, u, prev, tt=128):
    t, d = y.shape
    n = sum(r.shape[0] for r in rets)
    row = lambda c: pl.BlockSpec((tt, c), lambda i, *_: (i, 0))
    blk = pl.BlockSpec((tt*16, 128), lambda i, *_: (i, 0))
    return pl.pallas_call(functools.partial(_final_body, len(rets)),
        grid_spec=pltpu.PrefetchScalarGridSpec(num_scalar_prefetch=3, grid=(t//tt,),
            in_specs=[row(1), row(d), row(d), row(d)] + [pl.BlockSpec(memory_space=pl.ANY)]*len(rets) + [blk]*len(prev), out_specs=row(d),
            scratch_shapes=[pltpu.VMEM((n+16, 128), BF16), pltpu.VMEM((tt*16, 128), F32), pltpu.SemaphoreType.DMA((len(rets),))]),
        out_shape=jax.ShapeDtypeStruct((t, d), BF16), name="final",
        cost_estimate=pl.CostEstimate(flops=1024, bytes_accessed=2*n*128+24*t*d, transcendentals=0),
        compiler_params=pltpu.CompilerParams(dimension_semantics=("arbitrary",), vmem_limit_bytes=40<<20))(k, idx, w, zero, y, f, u, *rets, *prev)


def _rms(v, g):
    vf = v.astype(F32)
    return (vf * lax.rsqrt(jnp.mean(vf * vf, axis=-1, keepdims=True) + EPS) * g.astype(F32)).astype(BF16)


def _tables(pos):
    half = ROPE // 2
    ang = pos.astype(F32)[:, None] * (10000.0 ** (-jnp.arange(half, dtype=F32) / half))[None, :]
    cos, sin = jnp.cos(ang), jnp.sin(ang)
    z = jnp.zeros_like(sin)
    cat = lambda *a: jnp.concatenate(a, axis=1)
    return cat(cos, cos, z, z), cat(z, sin, z, z), cat(-sin, z, z, z)


def _after(v, *deps):
    return lax.optimization_barrier((v,) + deps)[0]


def solution(mesh):
    ncp = mesh.shape['cp']
    ngroup = mesh.shape['b'] * ncp
    axes = ('b', 'cp')
    tok = P(('dp', 'b'), 'cp', None)
    rep = P()
    espec = P(('b', 'cp'), None, None)

    def layer(x, ids, g_attn, w_q, w_dkv, w_kr, w_uk, w_uv, w_o, g_ffn, w_fg, w_fu, w_fd, g_moe, w_r, w_eg, w_eu, w_ed):
        rows, seq, d = x.shape
        top = ids.shape[-1]
        t = rows * seq
        epd = w_eg.shape[0]
        ne = epd * ngroup
        nslot = w_r.shape[1]
        hot = (nslot // top) // 2
        cap = (t + hot - 1) // hot
        i = lax.axis_index('cp')
        me = lax.axis_index('b') * ncp + i
        xt = x.reshape(t, d)
        tabs = _tables(i * seq + jnp.arange(seq))
        p = lax.axis_index('b')
        nb = ngroup // ncp
        idt = ids.reshape(t, top).T
        n, kv, logits, u = pre(xt, g_attn.reshape(1, d), g_moe.reshape(1, d), w_dkv, w_kr, w_r, tabs, 1)
        g = jax.nn.softmax(logits, axis=-1)
        oh = idt[:, :, None] == jnp.arange(nslot)
        sel = jnp.sum(jnp.where(oh, g[None], 0.0), axis=2)
        gate = sel / jnp.sum(sel, axis=0, keepdims=True)
        zero = jnp.sum(jnp.where(idt < ne, 0.0, gate), axis=0)
        meta = lax.all_gather(jnp.concatenate([idt.astype(F32), gate]), axes)
        meta, u = lax.optimization_barrier((meta, u))
        ua = lax.all_gather(u, axes)
        ida = meta[:, :top].astype(jnp.int32)

        def hop(v, *pairs):
            return lax.ppermute(v, 'b', list(pairs))

        far = lax.ppermute(kv, 'cp', [(0, 2), (1, 3)])
        near = lax.ppermute(kv, 'cp', [(0, 1), (2, 3)])
        kvs = [kv, far, near, lax.ppermute(far, 'cp', [(2, 3), (3, 2)])]
        home = [p] + [jnp.asarray(v, jnp.int32)[p] for v in ([3, 0, 3, 0], [2, 3, 0, 1], [1, 2, 1, 2])]
        k = jnp.arange(t)
        tri = (k[:, None] < k[None, :]).astype(BF16)
        hit = jnp.any(ida[:, None] == (epd * me + jnp.arange(epd))[None, :, None, None], axis=2)
        idl = jnp.stack([lax.dynamic_index_in_dim(ida, h * ncp + i, 0, keepdims=False) for h in home])
        gl = jnp.stack([lax.dynamic_index_in_dim(meta, h * ncp + i, 0, keepdims=False) for h in home])[:, top:]
        npl = epd * ncp
        x16 = idl - npl * p
        onp = (x16 >= 0) & (x16 < npl)
        ohl = x16[:, None] == jnp.arange(npl)[None, :, None, None]
        hitl = jnp.any(ohl, axis=2)
        both = jnp.concatenate([hit.reshape(-1, t), hitl.reshape(-1, t)]).astype(BF16)
        before = jnp.dot(both, tri, preferred_element_type=F32).astype(jnp.int32)
        rank = jnp.where(hit, before[:ngroup * epd].reshape(ngroup, epd, t), -1)
        some = jnp.any(hit, axis=2)
        rk = jnp.sum(jnp.where(ohl, before[ngroup * epd:].reshape(nb, npl, 1, t), 0), axis=1)
        nh = 2
        eh = epd // nh
        halved = x16 % epd // eh * (npl // nh) + x16 // epd * eh + x16 % eh
        xs = jnp.concatenate([x16[:1], halved[1:2], x16[2:]])
        row = jnp.where(onp, xs * cap + rk, npl * cap)
        wgt = jnp.where(onp, gl, 0.0)
        seen = jnp.cumsum(onp.astype(jnp.int32), axis=1)
        kmax = jnp.max(seen[:, -1], axis=1)
        put = onp[:, None] & (seen[:, None] - 1 == jnp.arange(top)[None, :, None, None])
        row = jnp.sum(jnp.where(put, row[:, None] - npl * cap, 0), axis=2) + npl * cap
        wgt = jnp.sum(jnp.where(put, wgt[:, None], 0.0), axis=2)
        def heads(k, dep):
            return attn(_after(i.reshape(1), dep), q, kvs, w_uv, k, 4)

        def rows_of(k, dep, parts=1):
            h = home[k]
            hs = _after(jnp.stack([h * ncp, h * ncp]), dep)
            xg = pick(hs, rank, ua, ncp, cap)
            full = lax.dynamic_slice_in_dim(some, h * ncp, ncp, 0)
            lst = jnp.argsort(~full, axis=0, stable=True).astype(jnp.int32).T.reshape(-1)
            num = jnp.sum(full, axis=0, dtype=jnp.int32)
            c = epd // parts
            outs = []
            for e in range(0, epd, c):
                outs.append(expert(e, c, _after(num, *outs), lst, xg, w_eg, w_eu, w_ed))
            return outs

        def back(k, outs):
            rets = []
            for o in outs:
                o = _after(o, *rets)
                rets.append(lax.all_to_all(o.reshape(ncp, -1, 128), 'cp', 0, 0).reshape(-1, 128))
            return jnp.maximum(kmax[k], 1).reshape(1), row[k].reshape(-1), wgt[k].reshape(-1), rets

        q = qproj(n, w_q, w_uk, tabs)
        oa = heads(0, q)
        ob = heads(1, oa)
        oc = heads(2, ob)
        o1 = rows_of(1, oc, 2)
        a1 = back(1, o1)
        od = heads(3, o1[-1])
        s1 = part(_after(a1[0], od), *a1[1:], [], t)
        r1 = hop(s1, (3, 2), (0, 1))
        o2 = rows_of(2, s1)
        a2 = back(2, o2)
        o3 = rows_of(3, o2[-1])
        o = _after(jnp.concatenate([oa, ob, oc, od], axis=1), o3[-1])
        a = jnp.dot(o, w_o, preferred_element_type=F32).astype(BF16)
        y = (xt.astype(F32) + a.astype(F32)).astype(BF16)
        o0 = rows_of(0, y)
        a3 = back(3, o3)
        z2 = _rms(_after(y, o0[-1]), g_ffn)
        hg = jax.nn.silu(jnp.dot(z2, w_fg, preferred_element_type=F32))
        s2 = part(_after(a2[0], hg), *a2[1:], [r1], t)
        r2a, r2b = hop(s2, (2, 1), (1, 2)), hop(s2, (3, 2), (0, 1))
        hid = (hg * jnp.dot(_after(z2, s2), w_fu, preferred_element_type=F32)).astype(BF16)
        s3 = part(_after(a3[0], hid), *a3[1:], [r2b], t)
        rc = hop(s1 + r2a, (1, 0), (2, 3))
        rd, re = hop(s3, (1, 2), (2, 1)), hop(s3, (0, 1), (3, 2))
        a0 = back(0, o0)
        f = jnp.dot(_after(hid, s3), w_fd, preferred_element_type=F32).astype(BF16)
        h = final(*a0, zero[:, None], y, f, u, [rc, rd, re])
        return h.reshape(rows, seq, d)

    return jax.shard_map(layer, mesh=mesh, in_specs=(tok, tok) + (rep,) * 13 + (espec,) * 3, out_specs=tok, check_vma=False)
```

time: 2070 us -> 1330 us (0.64)
  matrix products: 927 us -> 191 us
  Pallas kernels: 0 us -> 571 us
  waiting for transfers between devices: 710 us -> 362 us
  other arithmetic: 211 us -> 34.4 us
  local copies, waits for them, and re-layouts: 195 us -> 48.7 us
  starting transfers between devices: 16.7 us -> 74.5 us
  blocking collectives: 0 us -> 21.5 us
    dot_general x24 -> x5, matrix products: 927 us -> 191 us  [the longest x1 61.7 us: layer(): jnp.dot(_after(z2, s2), w_fu, preferred_element_type=F32)]
    all_to_all x2 -> x5, waiting for transfers between devices: 710 us -> 64.3 us  [back(): lax.all_to_all(o.reshape(ncp, -1, 128), 'cp', 0, 0).reshape(-1, 128)]
    pallas_call x0 -> x19, Pallas kernels: none -> 571 us  [the longest x4 267 us: attn(): pl.pallas_call(functools.partial(_attn_body, tq, sub), grid_spec=pltpu.Pr...]
    ppermute x3 -> x9, waiting for transfers between devices: 0.01 us -> 229 us  [the longest x6 229 us: hop(): return lax.ppermute(v, 'b', list(pairs))]
    reduce_sum x8 -> x7, other arithmetic: 86.9 us -> 3.96 us  [the longest x1 1.63 us: rows_of(): num = jnp.sum(full, axis=0, dtype=jnp.int32)]
    convert_element_type x3 -> x5, other arithmetic: 75.6 us -> 4.31 us  [the longest x1 3.2 us: _rms(): (vf * lax.rsqrt(jnp.mean(vf * vf, axis=-1, keepdims=True) + EPS) * g.asty...]
    all_gather x0 -> x1, waiting for transfers between devices: none -> 68.9 us  [layer(): ua = lax.all_gather(u, axes)]
    broadcast_in_dim x2, local copies, waits for them, and re-layouts: 57.4 us -> 0.22 us  [the longest x1 0.22 us: layer(): h = final(*a0, zero[:, None], y, f, u, [rc, rd, re])]
  transfers between devices with their start and end apart: 5 -> 15, of which waited for: 1 -> 8; matrix products, arithmetic and copies ran while one was open for 52% -> 17% of each run, Pallas kernels for 0% -> 33%
where the time goes in v1:
time: 1330 us; the launch traced here: 1320 us
  Pallas kernels  571 us (43%)
  waiting for transfers between devices  362 us (27%)
  matrix products  191 us (14%)
  starting transfers between devices  74.5 us (6%)
  local copies, waits for them, and re-layouts  48.7 us (4%)
  other arithmetic  34.4 us (3%)
  blocking collectives  21.5 us (2%)
  between operations  19.1 us (1%)
    pallas_call x4, Pallas kernels, attn(): pl.pallas_call(functools.partial(_attn_body, tq, sub), grid_spec=pltpu.Pr...  267 us
    ppermute x6, waiting for transfers between devices, hop(): return lax.ppermute(v, 'b', list(pairs))  229 us
    pallas_call x5, Pallas kernels, expert(): pl.pallas_call(functools.partial(_expert_body, e0, ne), grid_spec=pltpu.P...  148 us
    all_gather x1, waiting for transfers between devices, layer(): ua = lax.all_gather(u, axes)  68.9 us
    all_to_all x5, waiting for transfers between devices, back(): lax.all_to_all(o.reshape(ncp, -1, 128), 'cp', 0, 0).reshape(-1, 128)  64.3 us
    dot_general x1, matrix products, layer(): jnp.dot(_after(z2, s2), w_fu, preferred_element_type=F32)  61.7 us
    dot_general x1, matrix products, layer(): f = jnp.dot(_after(hid, s3), w_fd, preferred_element_type=F32).astype(BF16)  58.9 us
    all_to_all x5, starting transfers between devices, back(): lax.all_to_all(o.reshape(ncp, -1, 128), 'cp', 0, 0).reshape(-1, 128)  54.9 us
  transfers between devices with their start and end apart: 15, of which 8 were waited for; matrix products, arithmetic and copies ran while one was open for 17% of the time, Pallas kernels for 33%

profile of v1, /device:TPU:15, one launch (start us, length us, event | category | flops | bytes accessed | tf_op | source)
XLA Modules:
  0.0 1322.1 jit_solution(15984498065567548233)
XLA Ops:
  32.6 21.5 %all-gather.2 = f32[16,12,1024]{2,1,0:T(8,128)} all-gather(f32[1,12,1024]{2,1,0:T(8,128)S(1)} %maximum_bitcast_fusion), channel_id=2, replica_groups=mesh['dp'=2,'b'=4,'cp'=4] {'b','cp'}, dimensions={0}, use_global_device_ids=true | all-gather | bytes 835584 | tf_op jit(solution)/shard_map/all_gather | solution.py:366
  60.5 30.4 %qproj.1.q_ref = bf16[16,1024,640]{2,1,0:T(8,128)(2,1)} custom-call(bf16[1024,2048]{1,0:T(8,128)(2,1)S(1)} %copy-done.8, bf16[2048,3072]{1,0:T(8,128)(2,1)} %w_ref.1, bf16[16,128,512]{2,1,0:T(8,128)(2,1)S(1)} %copy-done.11, f32[1024,128]{1,0:T(8,128)S(1)} %get-tuple-element.115.c_ref, f32[1024,128]{1,0:T(8,128)S(1)} %get-tuple-element.114.sa_ref, ...), custom_call_target="tpu_custom_call" | custom-call | flops 1024 | bytes 67108864 | tf_op jit(solution)/shard_map/qproj/pallas_call | solution.py:74
  112.2 66.8 %attn.4 = bf16[1024,512]{1,0:T(8,128)(2,1)} custom-call(s32[1]{0:T(128)} %bitcast.10.i_ref, bf16[16,1024,640]{2,1,0:T(8,128)(2,1)} %qproj.1.q_ref, bf16[1024,640]{1,0:T(8,128)(2,1)} %copy-done.5, bf16[1024,640]{1,0:T(8,128)(2,1)} %collective-permute-done.k1, bf16[1024,640]{1,0:T(8,128)(2,1)} %collective-permute-done.1.k2, bf16[1024,640]{1,0:T(8,128)(2,1)} %copy-done.14, ...), custom_call_target="tpu_custom_call" | custom-call | flops 1024 | bytes 5242880 | tf_op jit(solution)/shard_map/attn/pallas_call | solution.py:128
  179.0 67.0 %attn.5 = bf16[1024,512]{1,0:T(8,128)(2,1)} custom-call(s32[1]{0:T(128)} %bitcast.10.i_ref, bf16[16,1024,640]{2,1,0:T(8,128)(2,1)} %qproj.1.q_ref, bf16[1024,640]{1,0:T(8,128)(2,1)} %copy-done.5, bf16[1024,640]{1,0:T(8,128)(2,1)} %collective-permute-done.k1, bf16[1024,640]{1,0:T(8,128)(2,1)} %collective-permute-done.1.k2, bf16[1024,640]{1,0:T(8,128)(2,1)} %copy-done.14, ...), custom_call_target="tpu_custom_call" | custom-call | flops 1024 | bytes 5242880 | tf_op jit(solution)/shard_map/attn/pallas_call | solution.py:128
  246.0 66.8 %attn.6 = bf16[1024,512]{1,0:T(8,128)(2,1)} custom-call(s32[1]{0:T(128)} %bitcast.10.i_ref, bf16[16,1024,640]{2,1,0:T(8,128)(2,1)} %qproj.1.q_ref, bf16[1024,640]{1,0:T(8,128)(2,1)} %copy-done.5, bf16[1024,640]{1,0:T(8,128)(2,1)} %collective-permute-done.k1, bf16[1024,640]{1,0:T(8,128)(2,1)} %collective-permute-done.1.k2, bf16[1024,640]{1,0:T(8,128)(2,1)} %copy-done.14, ...), custom_call_target="tpu_custom_call" | custom-call | flops 1024 | bytes 5242880 | tf_op jit(solution)/shard_map/attn/pallas_call | solution.py:128
  312.8 68.9 %all-gather.5.cloned.1.call-done = bf16[16384,2048]{1,0:T(8,128)(2,1)} async-done(((bf16[1024,2048]{1,0:T(8,128)(2,1)}), bf16[16384,2048]{1,0:T(8,128)(2,1)}) %all-gather.5.cloned.1.call-update) | async-done | bytes 67108880 | tf_op jit(solution)/shard_map/all_gather | solution.py:368
  381.7 12.8 pick.4.x_hbm
  397.8 13.3 %expert.5 = bf16[16384,128]{1,0:T(8,128)(2,1)} custom-call(s32[4]{0:T(128)} %get-tuple-element.43.n_ref, s32[16]{0:T(128)} %reshape.233.lst_ref, bf16[4,4,128,2048]{3,2,1,0:T(8,128)(2,1)} %copy-done, bf16[4,2048,1408]{2,1,0:T(8,128)(2,1)} %wg_hbm.9, bf16[4,2048,1408]{2,1,0:T(8,128)(2,1)} %wu_hbm.9, bf16[4,1408,2048]{2,1,0:T(8,128)(2,1)} %wd_hbm.9), custom_call_target="tpu_custom_call" | custom-call | flops 1024 | bytes 85983232 | tf_op jit(solution)/shard_map/expert/pallas_call | solution.py:232
  411.0 16.6 %all-to-all-start = ((bf16[4,4096,128]{2,1,0:T(8,128)(2,1)}), bf16[4,4096,128]{2,1,0:T(8,128)(2,1)}, u32[]{:S(2)}, u32[]{:S(2)}) async-start(bf16[4,4096,128]{2,1,0:T(8,128)(2,1)} %bitcast.56), calls=%async_computation | async-start | bytes 8388608 | tf_op jit(solution)/shard_map/all_to_all | solution.py:424
  427.6 12.9 expert.6
  440.6 33.5 %all-to-all-done = bf16[4,4096,128]{2,1,0:T(8,128)(2,1)} async-done(((bf16[4,4096,128]{2,1,0:T(8,128)(2,1)}), bf16[4,4096,128]{2,1,0:T(8,128)(2,1)}, u32[]{:S(2)}, u32[]{:S(2)}) %all-to-all-start) | async-done | bytes 4194336 | tf_op jit(solution)/shard_map/all_to_all | solution.py:424
  491.2 66.9 %attn.7 = bf16[1024,512]{1,0:T(8,128)(2,1)} custom-call(s32[1]{0:T(128)} %bitcast.10.i_ref, bf16[16,1024,640]{2,1,0:T(8,128)(2,1)} %qproj.1.q_ref, bf16[1024,640]{1,0:T(8,128)(2,1)} %copy-done.5, bf16[1024,640]{1,0:T(8,128)(2,1)} %collective-permute-done.k1, bf16[1024,640]{1,0:T(8,128)(2,1)} %collective-permute-done.1.k2, bf16[1024,640]{1,0:T(8,128)(2,1)} %copy-done.14, ...), custom_call_target="tpu_custom_call" | custom-call | flops 1024 | bytes 5242880 | tf_op jit(solution)/shard_map/attn/pallas_call | solution.py:128
  558.1 10.7 part.3
  568.8 13.2 pick.5.x_hbm
  587.6 35.5 %expert.7 = bf16[32768,128]{1,0:T(8,128)(2,1)} custom-call(s32[4]{0:T(128)} %get-tuple-element.64.n_ref, s32[16]{0:T(128)} %reshape.236.lst_ref, bf16[4,4,128,2048]{3,2,1,0:T(8,128)(2,1)} %copy-done.3, bf16[4,2048,1408]{2,1,0:T(8,128)(2,1)} %wg_hbm.9, bf16[4,2048,1408]{2,1,0:T(8,128)(2,1)} %wu_hbm.9, bf16[4,1408,2048]{2,1,0:T(8,128)(2,1)} %wd_hbm.9), custom_call_target="tpu_custom_call" | custom-call | flops 1024 | bytes 85983232 | tf_op jit(solution)/shard_map/expert/pallas_call | solution.py:232
  623.1 12.6 pick.6.x_hbm
  640.3 50.1 %expert.8 = bf16[32768,128]{1,0:T(8,128)(2,1)} custom-call(s32[4]{0:T(128)} %get-tuple-element.65.n_ref, s32[16]{0:T(128)} %reshape.235.lst_ref, bf16[4,4,128,2048]{3,2,1,0:T(8,128)(2,1)} %copy-done.4, bf16[4,2048,1408]{2,1,0:T(8,128)(2,1)} %wg_hbm.9, bf16[4,2048,1408]{2,1,0:T(8,128)(2,1)} %wu_hbm.9, bf16[4,1408,2048]{2,1,0:T(8,128)(2,1)} %wd_hbm.9), custom_call_target="tpu_custom_call" | custom-call | flops 1024 | bytes 85983232 | tf_op jit(solution)/shard_map/expert/pallas_call | solution.py:232
  690.4 14.5 %add_convert_fusion.y_ref = bf16[1024,2048]{1,0:T(8,128)(2,1)} fusion(bf16[1024,2048]{1,0:T(8,128)(2,1)} %pad_maximum_fusion, bf16[2048,2048]{1,0:T(8,128)(2,1)} %param.29, bf16[1,1024,2048]{2,1,0:T(8,128)(2,1)} %param.21), kind=kOutput, calls=%fused_computation.7 | convolution fusion | flops 8600420352 | bytes 20971520 | tf_op jit(solution)/shard_map/dot_general | solution.py:440
  704.9 12.6 pick.7.x_hbm
  726.5 36.7 %expert.9 = bf16[32768,128]{1,0:T(8,128)(2,1)} custom-call(s32[4]{0:T(128)} %get-tuple-element.63.n_ref, s32[16]{0:T(128)} %reshape.241.lst_ref, bf16[4,4,128,2048]{3,2,1,0:T(8,128)(2,1)} %copy-done.2, bf16[4,2048,1408]{2,1,0:T(8,128)(2,1)} %wg_hbm.9, bf16[4,2048,1408]{2,1,0:T(8,128)(2,1)} %wu_hbm.9, bf16[4,1408,2048]{2,1,0:T(8,128)(2,1)} %wd_hbm.9), custom_call_target="tpu_custom_call" | custom-call | flops 1024 | bytes 85983232 | tf_op jit(solution)/shard_map/expert/pallas_call | solution.py:232
  771.3 54.5 %fusion.40 = f32[1024,10944]{0,1:T(8,128)} fusion(bf16[1024,2048]{1,0:T(8,128)(2,1)S(1)} %fusion.2, bf16[2048,10944]{0,1:T(8,128)(2,1)} %param.31), kind=kOutput, calls=%fused_computation.118 | convolution fusion | flops 45902462976 | bytes 93847552 | tf_op jit(solution)/shard_map/dot_general | solution.py:445
  825.8 20.3 %all-to-all-start.3 = ((bf16[4,8192,128]{2,1,0:T(8,128)(2,1)}), bf16[4,8192,128]{2,1,0:T(8,128)(2,1)}, u32[]{:S(2)}, u32[]{:S(2)}) async-start(bf16[4,8192,128]{2,1,0:T(8,128)(2,1)} %bitcast.53), calls=%async_computation.3 | async-start | bytes 16777216 | tf_op jit(solution)/shard_map/all_to_all | solution.py:424
  846.1 15.3 %part.4 = f32[16384,128]{1,0:T(8,128)} custom-call(s32[1]{0:T(128)S(6)} %max.20.k_ref, s32[6144]{0:T(1024)S(1)} %reshape_squeeze.28.idx_ref, f32[6144]{0:T(1024)S(1)} %bitcast.50, bf16[32768,128]{1,0:T(8,128)(2,1)} %bitcast.24.rest_0_, f32[16384,128]{1,0:T(8,128)} %collective-permute-done.3.rest_1_), custom_call_target="tpu_custom_call" | custom-call | flops 1024 | bytes 33554432 | tf_op jit(solution)/shard_map/part/pallas_call | solution.py:282
  864.9 61.7 %multiply_convert_fusion = bf16[1024,10944]{0,1:T(8,128)(2,1)} fusion(bf16[1024,2048]{1,0:T(8,128)(2,1)} %copy-done.15, bf16[2048,10944]{0,1:T(8,128)(2,1)} %param.32, f32[1024,10944]{0,1:T(8,128)} %fusion.40), kind=kOutput, calls=%fused_computation | convolution fusion | flops 45969702912 | bytes 116260864 | tf_op jit(solution)/shard_map/dot_general | solution.py:448
  926.6 116.3 %collective-permute-done.5 = f32[16384,128]{1,0:T(8,128)} collective-permute-done((f32[16384,128]{1,0:T(8,128)}, f32[16384,128]{1,0:T(8,128)}, u32[]{:S(2)}, u32[]{:S(2)}) %collective-permute-start.5) | collective-permute-done | bytes 8388640 | tf_op jit(solution)/shard_map/ppermute | solution.py:372
  1057.1 27.2 %collective-permute-done.4.rest_1_ = f32[16384,128]{1,0:T(8,128)} collective-permute-done((f32[16384,128]{1,0:T(8,128)}, f32[16384,128]{1,0:T(8,128)}, u32[]{:S(2)}, u32[]{:S(2)}) %collective-permute-start.4) | collective-permute-done | bytes 8388640 | tf_op jit(solution)/shard_map/ppermute | solution.py:372
  1084.3 15.4 %part.5 = f32[16384,128]{1,0:T(8,128)} custom-call(s32[1]{0:T(128)S(6)} %max.21.k_ref, s32[6144]{0:T(1024)S(1)} %reshape_squeeze.30.idx_ref, f32[6144]{0:T(1024)S(1)} %bitcast.49, bf16[32768,128]{1,0:T(8,128)(2,1)} %bitcast.27.rest_0_, f32[16384,128]{1,0:T(8,128)} %collective-permute-done.4.rest_1_), custom_call_target="tpu_custom_call" | custom-call | flops 1024 | bytes 33554432 | tf_op jit(solution)/shard_map/part/pallas_call | solution.py:282
  1109.7 58.9 %convolution_convert_fusion.f_ref = bf16[1024,2048]{1,0:T(8,128)(2,1)} fusion(bf16[1024,10944]{0,1:T(8,128)(2,1)} %multiply_convert_fusion, bf16[10944,2048]{1,0:T(8,128)(2,1)} %param.33), kind=kOutput, calls=%fused_computation.11 | convolution fusion | flops 45904560128 | bytes 71434240 | tf_op jit(solution)/shard_map/dot_general | solution.py:453
  1168.5 30.8 %all-to-all-done.4 = bf16[4,8192,128]{2,1,0:T(8,128)(2,1)} async-done(((bf16[4,8192,128]{2,1,0:T(8,128)(2,1)}), bf16[4,8192,128]{2,1,0:T(8,128)(2,1)}, u32[]{:S(2)}, u32[]{:S(2)}) %all-to-all-start.4) | async-done | bytes 8388640 | tf_op jit(solution)/shard_map/all_to_all | solution.py:424
  1199.3 31.3 %collective-permute-done.6.rest_1_ = f32[16384,128]{1,0:T(8,128)} collective-permute-done((f32[16384,128]{1,0:T(8,128)}, f32[16384,128]{1,0:T(8,128)}, u32[]{:S(2)}, u32[]{:S(2)}) %collective-permute-start.6) | collective-permute-done | bytes 8388640 | tf_op jit(solution)/shard_map/ppermute | solution.py:372
  1230.7 52.3 %collective-permute-done.7.rest_2_ = f32[16384,128]{1,0:T(8,128)} collective-permute-done((f32[16384,128]{1,0:T(8,128)}, f32[16384,128]{1,0:T(8,128)}, u32[]{:S(2)}, u32[]{:S(2)}) %collective-permute-start.7) | collective-permute-done | bytes 8388640 | tf_op jit(solution)/shard_map/ppermute | solution.py:372
  1291.5 23.3 %final.1 = bf16[1024,2048]{1,0:T(8,128)(2,1)} custom-call(s32[1]{0:T(128)S(6)} %max.18.k_ref, s32[6144]{0:T(1024)S(1)} %reshape_squeeze.24.idx_ref, f32[6144]{0:T(1024)S(1)} %bitcast.48, f32[1024,1]{1,0:T(8,128)S(1)} %copy.76.z_ref, bf16[1024,2048]{1,0:T(8,128)(2,1)S(1)} %copy-done.1, bf16[1024,2048]{1,0:T(8,128)(2,1)S(1)} %copy-done.9, ...), custom_call_target="tpu_custom_call" | custom-call | flops 1024 | bytes 58720256 | tf_op jit(solution)/shard_map/final/pallas_call | solution.py:309
  (186 shorter events, 132.5 us)
Async XLA Ops:
  6.5 375.2 %all-gather.5.cloned.1.call-start = ((), (), s32[]{:S(2)}) async-start(), calls=%async_computation.5 | async-start | bytes 71303168 | tf_op jit(solution)/shard_map/all_gather | solution.py:368
  8.6 22.9 %copy-start.24 = (s32[1,1024,6]{1,0,2:T(1,128)S(1)}, s32[1,1024,6]{1,0,2:T(1,128)}, u32[]{:S(2)}) copy-start(s32[1,1024,6]{1,0,2:T(1,128)} %param.22) | copy-start | bytes 73732
  28.5 62.4 %copy-start.5 = (bf16[1024,640]{1,0:T(8,128)(2,1)}, bf16[1024,640]{1,0:T(8,128)(2,1)S(1)}, u32[]{:S(2)}) copy-start(bf16[1024,640]{1,0:T(8,128)(2,1)S(1)} %get-tuple-element.37.k0) | copy-start | bytes 3932164
  54.1 43.6 %collective-permute-start = (bf16[1024,640]{1,0:T(8,128)(2,1)S(1)}, bf16[1024,640]{1,0:T(8,128)(2,1)}, u32[]{:S(2)}, u32[]{:S(2)}) collective-permute-start(bf16[1024,640]{1,0:T(8,128)(2,1)S(1)} %get-tuple-element.37.k0), channel_id=1, source_target_pairs={{0,2},{1,3},{4,6},{5,7},{8,10},{9,11},{12,14},{13,15},{16,18},{17,... | collective-permute-start | bytes 3932168 | tf_op jit(solution)/shard_map/ppermute | solution.py:374
  55.4 55.7 %collective-permute-start.1 = (bf16[1024,640]{1,0:T(8,128)(2,1)S(1)}, bf16[1024,640]{1,0:T(8,128)(2,1)}, u32[]{:S(2)}, u32[]{:S(2)}) collective-permute-start(bf16[1024,640]{1,0:T(8,128)(2,1)S(1)} %get-tuple-element.37.k0), channel_id=1, source_target_pairs={{0,1},{2,3},{4,5},{6,7},{8,9},{10,11},{12,13},{14,15},{16,17},{18,... | collective-permute-start | bytes 3932168 | tf_op jit(solution)/shard_map/ppermute | solution.py:375
  60.5 30.4 %copy-start.33 = (s32[4]{0:T(128)S(1)}, s32[4]{0:T(128)}, u32[]{:S(2)}) copy-start(s32[4]{0:T(128)} %constant.139.clone) | copy-start | bytes 52
  60.5 31.6 %copy-start.32 = (s32[4]{0:T(128)S(1)}, s32[4]{0:T(128)}, u32[]{:S(2)}) copy-start(s32[4]{0:T(128)} %constant.140.clone) | copy-start | bytes 52
  60.5 32.8 %copy-start.31 = (s32[4]{0:T(128)S(1)}, s32[4]{0:T(128)}, u32[]{:S(2)}) copy-start(s32[4]{0:T(128)} %constant.141.clone) | copy-start | bytes 52
  97.7 13.4 %collective-permute-start.2 = (bf16[1024,640]{1,0:T(8,128)(2,1)}, bf16[1024,640]{1,0:T(8,128)(2,1)S(1)}, u32[]{:S(2)}, u32[]{:S(2)}) collective-permute-start(bf16[1024,640]{1,0:T(8,128)(2,1)} %collective-permute-done.k1), channel_id=1, source_target_pairs={{2,3},{3,2},{6,7},{7,6},{10,11},{11,10},{14,15},{15,14},{18,19},{1... | collective-permute-start | bytes 3932168 | tf_op jit(solution)/shard_map/ppermute | solution.py:376
  411.0 63.1 %all-to-all-start = ((bf16[4,4096,128]{2,1,0:T(8,128)(2,1)}), bf16[4,4096,128]{2,1,0:T(8,128)(2,1)}, u32[]{:S(2)}, u32[]{:S(2)}) async-start(bf16[4,4096,128]{2,1,0:T(8,128)(2,1)} %bitcast.56), calls=%async_computation | async-start | bytes 8388608 | tf_op jit(solution)/shard_map/all_to_all | solution.py:424
  440.6 40.1 %copy-start.22 = (pred[4,6,1024]{2,1,0:T(8,128)(4,1)S(1)}, pred[4,6,1024]{2,1,0:T(8,128)(4,1)}, u32[]{:S(2)}) copy-start(pred[4,6,1024]{2,1,0:T(8,128)(4,1)} %get-tuple-element.70) | copy-start | bytes 73732
  440.6 40.4 %copy-start.21 = (f32[4,6,1024]{2,1,0:T(8,128)S(1)}, f32[4,6,1024]{2,1,0:T(8,128)}, u32[]{:S(2)}) copy-start(f32[4,6,1024]{2,1,0:T(8,128)} %get-tuple-element.69) | copy-start | bytes 294916
  440.6 40.5 %copy-start.20 = (s32[64,1024]{1,0:T(8,128)S(1)}, s32[64,1024]{1,0:T(8,128)}, u32[]{:S(2)}) copy-start(s32[64,1024]{1,0:T(8,128)} %get-tuple-element.77) | copy-start | bytes 786436
  440.6 42.2 %copy-start.30 = (pred[4,4]{0,1:T(4,128)(4,1)S(1)}, pred[4,4]{0,1:T(4,128)(4,1)}, u32[]{:S(2)}) copy-start(pred[4,4]{0,1:T(4,128)(4,1)} %get-tuple-element.112) | copy-start | bytes 52
  440.6 45.9 %copy-start.29 = (pred[4,4]{0,1:T(4,128)(4,1)S(1)}, pred[4,4]{0,1:T(4,128)(4,1)}, u32[]{:S(2)}) copy-start(pred[4,4]{0,1:T(4,128)(4,1)} %get-tuple-element.113) | copy-start | bytes 52
  440.6 47.4 %copy-start.28 = (pred[4,4]{0,1:T(4,128)(4,1)S(1)}, pred[4,4]{0,1:T(4,128)(4,1)}, u32[]{:S(2)}) copy-start(pred[4,4]{0,1:T(4,128)(4,1)} %get-tuple-element.110) | copy-start | bytes 52
  440.6 48.7 %copy-start.27 = (bf16[2048]{0:T(1024)(128)(2,1)S(1)}, bf16[2048]{0:T(1024)(128)(2,1)}, u32[]{:S(2)}) copy-start(bf16[2048]{0:T(1024)(128)(2,1)} %param.30) | copy-start | bytes 12292
  474.1 84.0 %all-to-all-start.1 = ((bf16[4,4096,128]{2,1,0:T(8,128)(2,1)}), bf16[4,4096,128]{2,1,0:T(8,128)(2,1)}, u32[]{:S(2)}, u32[]{:S(2)}) async-start(bf16[4,4096,128]{2,1,0:T(8,128)(2,1)} %bitcast.55), calls=%async_computation.1 | async-start | bytes 8388608 | tf_op jit(solution)/shard_map/all_to_all | solution.py:424
  568.8 16.5 %copy-start.16 = (bf16[1024,512]{1,0:T(8,128)(2,1)S(1)}, bf16[1024,512]{1,0:T(8,128)(2,1)}, u32[]{:S(2)}) copy-start(bf16[1024,512]{1,0:T(8,128)(2,1)} %attn.4) | copy-start | bytes 3145732
  568.8 16.5 %copy-start.17 = (bf16[1024,512]{1,0:T(8,128)(2,1)S(1)}, bf16[1024,512]{1,0:T(8,128)(2,1)}, u32[]{:S(2)}) copy-start(bf16[1024,512]{1,0:T(8,128)(2,1)} %attn.5) | copy-start | bytes 3145732
  568.8 16.5 %copy-start.18 = (bf16[1024,512]{1,0:T(8,128)(2,1)S(1)}, bf16[1024,512]{1,0:T(8,128)(2,1)}, u32[]{:S(2)}) copy-start(bf16[1024,512]{1,0:T(8,128)(2,1)} %attn.6) | copy-start | bytes 3145732
  568.8 16.5 %copy-start.19 = (bf16[1024,512]{1,0:T(8,128)(2,1)S(1)}, bf16[1024,512]{1,0:T(8,128)(2,1)}, u32[]{:S(2)}) copy-start(bf16[1024,512]{1,0:T(8,128)(2,1)} %attn.7) | copy-start | bytes 3145732
  639.0 207.0 %collective-permute-start.3 = (f32[16384,128]{1,0:T(8,128)}, f32[16384,128]{1,0:T(8,128)}, u32[]{:S(2)}, u32[]{:S(2)}) collective-permute-start(f32[16384,128]{1,0:T(8,128)} %part.3), channel_id=1, source_target_pairs={{12,8},{0,4},{13,9},{1,5},{14,10},{2,6},{15,11},{3,7},{28,24},{16,... | collective-permute-start | bytes 25165832 | tf_op jit(solution)/shard_map/ppermute | solution.py:372
  720.8 105.0 %all-to-all-start.2 = ((bf16[4,8192,128]{2,1,0:T(8,128)(2,1)}), bf16[4,8192,128]{2,1,0:T(8,128)(2,1)}, u32[]{:S(2)}, u32[]{:S(2)}) async-start(bf16[4,8192,128]{2,1,0:T(8,128)(2,1)} %bitcast.54), calls=%async_computation.2 | async-start | bytes 16777216 | tf_op jit(solution)/shard_map/all_to_all | solution.py:424
  726.4 39.8 %copy-start.25 = (f32[2048]{0:T(1024)S(1)}, f32[2048]{0:T(1024)}, u32[]{:S(2)}) copy-start(f32[2048]{0:T(1024)} %convert_element_type.74) | copy-start | bytes 24580
  825.8 231.3 %all-to-all-start.3 = ((bf16[4,8192,128]{2,1,0:T(8,128)(2,1)}), bf16[4,8192,128]{2,1,0:T(8,128)(2,1)}, u32[]{:S(2)}, u32[]{:S(2)}) async-start(bf16[4,8192,128]{2,1,0:T(8,128)(2,1)} %bitcast.53), calls=%async_computation.3 | async-start | bytes 16777216 | tf_op jit(solution)/shard_map/all_to_all | solution.py:424
  861.4 181.5 %collective-permute-start.5 = (f32[16384,128]{1,0:T(8,128)}, f32[16384,128]{1,0:T(8,128)}, u32[]{:S(2)}, u32[]{:S(2)}) collective-permute-start(f32[16384,128]{1,0:T(8,128)} %part.4), channel_id=1, source_target_pairs={{8,4},{4,8},{9,5},{5,9},{10,6},{6,10},{11,7},{7,11},{24,20},{20,24... | collective-permute-start | bytes 25165832 | tf_op jit(solution)/shard_map/ppermute | solution.py:372
  863.3 221.0 %collective-permute-start.4 = (f32[16384,128]{1,0:T(8,128)}, f32[16384,128]{1,0:T(8,128)}, u32[]{:S(2)}, u32[]{:S(2)}) collective-permute-start(f32[16384,128]{1,0:T(8,128)} %part.4), channel_id=1, source_target_pairs={{12,8},{0,4},{13,9},{1,5},{14,10},{2,6},{15,11},{3,7},{28,24},{16,... | collective-permute-start | bytes 25165832 | tf_op jit(solution)/shard_map/ppermute | solution.py:372
  1052.6 178.1 %collective-permute-start.6 = (f32[16384,128]{1,0:T(8,128)}, f32[16384,128]{1,0:T(8,128)}, u32[]{:S(2)}, u32[]{:S(2)}) collective-permute-start(f32[16384,128]{1,0:T(8,128)} %add.163), channel_id=1, source_target_pairs={{4,0},{8,12},{5,1},{9,13},{6,2},{10,14},{7,3},{11,15},{20,16},{24,... | collective-permute-start | bytes 25165832 | tf_op jit(solution)/shard_map/ppermute | solution.py:372
  1099.7 183.3 %collective-permute-start.7 = (f32[16384,128]{1,0:T(8,128)}, f32[16384,128]{1,0:T(8,128)}, u32[]{:S(2)}, u32[]{:S(2)}) collective-permute-start(f32[16384,128]{1,0:T(8,128)} %part.5), channel_id=1, source_target_pairs={{4,8},{8,4},{5,9},{9,5},{6,10},{10,6},{7,11},{11,7},{20,24},{24,20... | collective-permute-start | bytes 25165832 | tf_op jit(solution)/shard_map/ppermute | solution.py:372
  1101.7 183.3 %collective-permute-start.8 = (f32[16384,128]{1,0:T(8,128)}, f32[16384,128]{1,0:T(8,128)}, u32[]{:S(2)}, u32[]{:S(2)}) collective-permute-start(f32[16384,128]{1,0:T(8,128)} %part.5), channel_id=1, source_target_pairs={{0,4},{12,8},{1,5},{13,9},{2,6},{14,10},{3,7},{15,11},{16,20},{28,... | collective-permute-start | bytes 25165832 | tf_op jit(solution)/shard_map/ppermute | solution.py:372
  1103.0 96.4 %all-to-all-start.4 = ((bf16[4,8192,128]{2,1,0:T(8,128)(2,1)}), bf16[4,8192,128]{2,1,0:T(8,128)(2,1)}, u32[]{:S(2)}, u32[]{:S(2)}) async-start(bf16[4,8192,128]{2,1,0:T(8,128)(2,1)} %bitcast.52), calls=%async_computation.4 | async-start | bytes 16777216 | tf_op jit(solution)/shard_map/all_to_all | solution.py:424
  (17 other events, 44.5 us)
Sparse Core Ops, SparseCore 0:
  54.2 327.4 all-gather.4

commit v2 on v1

--- a/solution.py
+++ b/solution.py
@@ -428,28 +428,28 @@
         oa = heads(0, q)
         ob = heads(1, oa)
         oc = heads(2, ob)
-        o1 = rows_of(1, oc, 2)
+        od = heads(3, oc)
+        o1 = rows_of(1, od, 2)
         a1 = back(1, o1)
-        od = heads(3, o1[-1])
-        s1 = part(_after(a1[0], od), *a1[1:], [], t)
+        o = _after(jnp.concatenate([oa, ob, oc, od], axis=1), o1[-1])
+        a = jnp.dot(o, w_o, preferred_element_type=F32).astype(BF16)
+        y = (xt.astype(F32) + a.astype(F32)).astype(BF16)
+        s1 = part(_after(a1[0], y), *a1[1:], [], t)
         r1 = hop(s1, (3, 2), (0, 1))
         o2 = rows_of(2, s1)
         a2 = back(2, o2)
         o3 = rows_of(3, o2[-1])
-        o = _after(jnp.concatenate([oa, ob, oc, od], axis=1), o3[-1])
-        a = jnp.dot(o, w_o, preferred_element_type=F32).astype(BF16)
-        y = (xt.astype(F32) + a.astype(F32)).astype(BF16)
-        o0 = rows_of(0, y)
-        a3 = back(3, o3)
-        z2 = _rms(_after(y, o0[-1]), g_ffn)
+        o0 = rows_of(0, o3[-1])
+        s2 = part(_after(a2[0], o0[-1]), *a2[1:], [r1], t)
+        r2a, r2b = hop(s2, (2, 1), (1, 2)), hop(s2, (3, 2), (0, 1))
+        a3 = back(3, [_after(o3[-1], s2)])
+        z2 = _rms(_after(y, s2), g_ffn)
         hg = jax.nn.silu(jnp.dot(z2, w_fg, preferred_element_type=F32))
-        s2 = part(_after(a2[0], hg), *a2[1:], [r1], t)
-        r2a, r2b = hop(s2, (2, 1), (1, 2)), hop(s2, (3, 2), (0, 1))
-        hid = (hg * jnp.dot(_after(z2, s2), w_fu, preferred_element_type=F32)).astype(BF16)
+        hid = (hg * jnp.dot(_after(z2, hg), w_fu, preferred_element_type=F32)).astype(BF16)
         s3 = part(_after(a3[0], hid), *a3[1:], [r2b], t)
         rc = hop(s1 + r2a, (1, 0), (2, 3))
         rd, re = hop(s3, (1, 2), (2, 1)), hop(s3, (0, 1), (3, 2))
-        a0 = back(0, o0)
+        a0 = back(0, [_after(o0[-1], s3)])
         f = jnp.dot(_after(hid, s3), w_fd, preferred_element_type=F32).astype(BF16)
         h = final(*a0, zero[:, None], y, f, u, [rc, rd, re])
         return h.reshape(rows, seq, d)

time: 1330 us -> 1230 us (0.925)
  the two profiles are of different devices: /device:TPU:15 before, /device:TPU:1 now
where the time goes in v2:
time: 1230 us; the launch traced here: 1220 us
  Pallas kernels  500 us (41%)
  waiting for transfers between devices  336 us (27%)
  matrix products  189 us (15%)
  starting transfers between devices  66.8 us (5%)
  local copies, waits for them, and re-layouts  50.9 us (4%)
  other arithmetic  32.1 us (3%)
  blocking collectives  27.4 us (2%)
  between operations  19.1 us (2%)
    pallas_call x5, Pallas kernels, expert(): pl.pallas_call(functools.partial(_expert_body, e0, ne), grid_spec=pltpu.P...  211 us
    all_gather x1, waiting for transfers between devices, layer(): ua = lax.all_gather(u, axes)  147 us
    pallas_call x4, Pallas kernels, attn(): pl.pallas_call(functools.partial(_attn_body, tq, sub), grid_spec=pltpu.Pr...  133 us
    ppermute x6, waiting for transfers between devices, hop(): return lax.ppermute(v, 'b', list(pairs))  97.3 us
    all_to_all x5, waiting for transfers between devices, back(): lax.all_to_all(o.reshape(ncp, -1, 128), 'cp', 0, 0).reshape(-1, 128)  81.3 us
    dot_general x1, matrix products, layer(): jnp.dot(_after(z2, hg), w_fu, preferred_element_type=F32)  62.1 us
    dot_general x1, matrix products, layer(): f = jnp.dot(_after(hid, s3), w_fd, preferred_element_type=F32).astype(BF16)  58.9 us
    dot_general x1, matrix products, layer(): hg = jax.nn.silu(jnp.dot(z2, w_fg, preferred_element_type=F32))  54.5 us
  transfers between devices with their start and end apart: 15, of which 8 were waited for; matrix products, arithmetic and copies ran while one was open for 18% of the time, Pallas kernels for 33%

profile of v2, /device:TPU:1, one launch (start us, length us, event | category | flops | bytes accessed | tf_op | source)
XLA Modules:
  0.0 1220.0 jit_solution(7551340300638575884)
XLA Ops:
  32.6 27.4 %all-gather.2 = f32[16,12,1024]{2,1,0:T(8,128)} all-gather(f32[1,12,1024]{2,1,0:T(8,128)S(1)} %maximum_bitcast_fusion), channel_id=2, replica_groups=mesh['dp'=2,'b'=4,'cp'=4] {'b','cp'}, dimensions={0}, use_global_device_ids=true | all-gather | bytes 835584 | tf_op jit(solution)/shard_map/all_gather | solution.py:366
  69.0 30.0 %qproj.1.q_ref = bf16[16,1024,640]{2,1,0:T(8,128)(2,1)} custom-call(bf16[1024,2048]{1,0:T(8,128)(2,1)S(1)} %copy-done.8, bf16[2048,3072]{1,0:T(8,128)(2,1)} %w_ref.1, bf16[16,128,512]{2,1,0:T(8,128)(2,1)S(1)} %copy-done.11, f32[1024,128]{1,0:T(8,128)S(1)} %get-tuple-element.119.c_ref, f32[1024,128]{1,0:T(8,128)S(1)} %get-tuple-element.118.sa_ref, ...), custom_call_target="tpu_custom_call" | custom-call | flops 1024 | bytes 67108864 | tf_op jit(solution)/shard_map/qproj/pallas_call | solution.py:74
  105.4 10.2 collective-permute-done.k1
  124.7 33.5 %attn.4 = bf16[1024,512]{1,0:T(8,128)(2,1)} custom-call(s32[1]{0:T(128)} %bitcast.10.i_ref, bf16[16,1024,640]{2,1,0:T(8,128)(2,1)} %qproj.1.q_ref, bf16[1024,640]{1,0:T(8,128)(2,1)} %copy-done.5, bf16[1024,640]{1,0:T(8,128)(2,1)} %collective-permute-done.k1, bf16[1024,640]{1,0:T(8,128)(2,1)} %collective-permute-done.1.k2, bf16[1024,640]{1,0:T(8,128)(2,1)} %copy-done.14, ...), custom_call_target="tpu_custom_call" | custom-call | flops 1024 | bytes 5242880 | tf_op jit(solution)/shard_map/attn/pallas_call | solution.py:128
  158.2 33.2 %attn.5 = bf16[1024,512]{1,0:T(8,128)(2,1)} custom-call(s32[1]{0:T(128)} %bitcast.10.i_ref, bf16[16,1024,640]{2,1,0:T(8,128)(2,1)} %qproj.1.q_ref, bf16[1024,640]{1,0:T(8,128)(2,1)} %copy-done.5, bf16[1024,640]{1,0:T(8,128)(2,1)} %collective-permute-done.k1, bf16[1024,640]{1,0:T(8,128)(2,1)} %collective-permute-done.1.k2, bf16[1024,640]{1,0:T(8,128)(2,1)} %copy-done.14, ...), custom_call_target="tpu_custom_call" | custom-call | flops 1024 | bytes 5242880 | tf_op jit(solution)/shard_map/attn/pallas_call | solution.py:128
  191.3 33.2 %attn.6 = bf16[1024,512]{1,0:T(8,128)(2,1)} custom-call(s32[1]{0:T(128)} %bitcast.10.i_ref, bf16[16,1024,640]{2,1,0:T(8,128)(2,1)} %qproj.1.q_ref, bf16[1024,640]{1,0:T(8,128)(2,1)} %copy-done.5, bf16[1024,640]{1,0:T(8,128)(2,1)} %collective-permute-done.k1, bf16[1024,640]{1,0:T(8,128)(2,1)} %collective-permute-done.1.k2, bf16[1024,640]{1,0:T(8,128)(2,1)} %copy-done.14, ...), custom_call_target="tpu_custom_call" | custom-call | flops 1024 | bytes 5242880 | tf_op jit(solution)/shard_map/attn/pallas_call | solution.py:128
  224.5 33.4 %attn.7 = bf16[1024,512]{1,0:T(8,128)(2,1)} custom-call(s32[1]{0:T(128)} %bitcast.10.i_ref, bf16[16,1024,640]{2,1,0:T(8,128)(2,1)} %qproj.1.q_ref, bf16[1024,640]{1,0:T(8,128)(2,1)} %copy-done.5, bf16[1024,640]{1,0:T(8,128)(2,1)} %collective-permute-done.k1, bf16[1024,640]{1,0:T(8,128)(2,1)} %collective-permute-done.1.k2, bf16[1024,640]{1,0:T(8,128)(2,1)} %copy-done.14, ...), custom_call_target="tpu_custom_call" | custom-call | flops 1024 | bytes 5242880 | tf_op jit(solution)/shard_map/attn/pallas_call | solution.py:128
  257.9 146.7 %all-gather.5.cloned.1.call-done = bf16[16384,2048]{1,0:T(8,128)(2,1)} async-done(((bf16[1024,2048]{1,0:T(8,128)(2,1)}), bf16[16384,2048]{1,0:T(8,128)(2,1)}) %all-gather.5.cloned.1.call-update) | async-done | bytes 67108880 | tf_op jit(solution)/shard_map/all_gather | solution.py:368
  404.6 12.8 %pick.4.x_hbm = bf16[4,4,128,2048]{3,2,1,0:T(8,128)(2,1)S(1)} custom-call(s32[2]{0:T(128)S(1)} %pad_add_fusion.h_ref, s32[16,4,1024]{2,1,0:T(4,128)S(1)} %broadcast_select_fusion.rank_ref, bf16[16,1024,2048]{2,1,0:T(8,128)(2,1)} %bitcast.12.u_ref), custom_call_target="tpu_custom_call" | custom-call | flops 1024 | bytes 25165824 | tf_op jit(solution)/shard_map/pick/pallas_call | solution.py:152
  420.6 21.2 %expert.5 = bf16[16384,128]{1,0:T(8,128)(2,1)} custom-call(s32[4]{0:T(128)} %get-tuple-element.46.n_ref, s32[16]{0:T(128)} %reshape.233.lst_ref, bf16[4,4,128,2048]{3,2,1,0:T(8,128)(2,1)} %copy-done, bf16[4,2048,1408]{2,1,0:T(8,128)(2,1)} %wg_hbm.9, bf16[4,2048,1408]{2,1,0:T(8,128)(2,1)} %wu_hbm.9, bf16[4,1408,2048]{2,1,0:T(8,128)(2,1)} %wd_hbm.9), custom_call_target="tpu_custom_call" | custom-call | flops 1024 | bytes 85983232 | tf_op jit(solution)/shard_map/expert/pallas_call | solution.py:232
  441.9 15.9 %all-to-all-start = ((bf16[4,4096,128]{2,1,0:T(8,128)(2,1)}), bf16[4,4096,128]{2,1,0:T(8,128)(2,1)}, u32[]{:S(2)}, u32[]{:S(2)}) async-start(bf16[4,4096,128]{2,1,0:T(8,128)(2,1)} %bitcast.55), calls=%async_computation | async-start | bytes 8388608 | tf_op jit(solution)/shard_map/all_to_all | solution.py:424
  459.8 22.0 %expert.6 = bf16[16384,128]{1,0:T(8,128)(2,1)} custom-call(s32[4]{0:T(128)} %get-tuple-element.46.n_ref, s32[16]{0:T(128)} %reshape.233.lst_ref, bf16[4,4,128,2048]{3,2,1,0:T(8,128)(2,1)} %copy-done, bf16[4,2048,1408]{2,1,0:T(8,128)(2,1)} %wg_hbm.9, bf16[4,2048,1408]{2,1,0:T(8,128)(2,1)} %wu_hbm.9, bf16[4,1408,2048]{2,1,0:T(8,128)(2,1)} %wd_hbm.9), custom_call_target="tpu_custom_call" | custom-call | flops 1024 | bytes 85983232 | tf_op jit(solution)/shard_map/expert/pallas_call | solution.py:232
  481.8 23.2 %all-to-all-done = bf16[4,4096,128]{2,1,0:T(8,128)(2,1)} async-done(((bf16[4,4096,128]{2,1,0:T(8,128)(2,1)}), bf16[4,4096,128]{2,1,0:T(8,128)(2,1)}, u32[]{:S(2)}, u32[]{:S(2)}) %all-to-all-start) | async-done | bytes 4194336 | tf_op jit(solution)/shard_map/all_to_all | solution.py:424
  516.0 12.6 %add_convert_fusion.y_ref = bf16[1024,2048]{1,0:T(8,128)(2,1)} fusion(bf16[1024,2048]{1,0:T(8,128)(2,1)S(1)} %pad_maximum_fusion, bf16[2048,2048]{1,0:T(8,128)(2,1)} %param.29, bf16[1,1024,2048]{2,1,0:T(8,128)(2,1)S(1)} %copy-done.15), kind=kOutput, calls=%fused_computation.7 | convolution fusion | flops 8600420352 | bytes 20971520 | tf_op jit(solution)/shard_map/dot_general | solution.py:435
  528.6 29.4 %all-to-all-done.1 = bf16[4,4096,128]{2,1,0:T(8,128)(2,1)} async-done(((bf16[4,4096,128]{2,1,0:T(8,128)(2,1)}), bf16[4,4096,128]{2,1,0:T(8,128)(2,1)}, u32[]{:S(2)}, u32[]{:S(2)}) %all-to-all-start.1) | async-done | bytes 4194336 | tf_op jit(solution)/shard_map/all_to_all | solution.py:424
  558.1 10.7 part.3
  574.9 12.6 %pick.5.x_hbm = bf16[4,4,128,2048]{3,2,1,0:T(8,128)(2,1)S(1)} custom-call(s32[2]{0:T(128)S(1)} %pad_add_fusion.3.h_ref, s32[16,4,1024]{2,1,0:T(4,128)S(1)} %broadcast_select_fusion.rank_ref, bf16[16,1024,2048]{2,1,0:T(8,128)(2,1)} %bitcast.12.u_ref), custom_call_target="tpu_custom_call" | custom-call | flops 1024 | bytes 25165824 | tf_op jit(solution)/shard_map/pick/pallas_call | solution.py:152
  590.7 55.9 %expert.7 = bf16[32768,128]{1,0:T(8,128)(2,1)} custom-call(s32[4]{0:T(128)} %get-tuple-element.67.n_ref, s32[16]{0:T(128)} %reshape.237.lst_ref, bf16[4,4,128,2048]{3,2,1,0:T(8,128)(2,1)} %copy-done.4, bf16[4,2048,1408]{2,1,0:T(8,128)(2,1)} %wg_hbm.9, bf16[4,2048,1408]{2,1,0:T(8,128)(2,1)} %wu_hbm.9, bf16[4,1408,2048]{2,1,0:T(8,128)(2,1)} %wd_hbm.9), custom_call_target="tpu_custom_call" | custom-call | flops 1024 | bytes 85983232 | tf_op jit(solution)/shard_map/expert/pallas_call | solution.py:232
  656.0 12.6 %pick.6.x_hbm = bf16[4,4,128,2048]{3,2,1,0:T(8,128)(2,1)S(1)} custom-call(s32[2]{0:T(128)S(1)} %get-tuple-element.54.h_ref, s32[16,4,1024]{2,1,0:T(4,128)S(1)} %broadcast_select_fusion.rank_ref, bf16[16,1024,2048]{2,1,0:T(8,128)(2,1)} %bitcast.12.u_ref), custom_call_target="tpu_custom_call" | custom-call | flops 1024 | bytes 25165824 | tf_op jit(solution)/shard_map/pick/pallas_call | solution.py:152
  672.4 56.1 %expert.8 = bf16[32768,128]{1,0:T(8,128)(2,1)} custom-call(s32[4]{0:T(128)} %get-tuple-element.68.n_ref, s32[16]{0:T(128)} %reshape.236.lst_ref, bf16[4,4,128,2048]{3,2,1,0:T(8,128)(2,1)} %copy-done.3, bf16[4,2048,1408]{2,1,0:T(8,128)(2,1)} %wg_hbm.9, bf16[4,2048,1408]{2,1,0:T(8,128)(2,1)} %wu_hbm.9, bf16[4,1408,2048]{2,1,0:T(8,128)(2,1)} %wd_hbm.9), custom_call_target="tpu_custom_call" | custom-call | flops 1024 | bytes 85983232 | tf_op jit(solution)/shard_map/expert/pallas_call | solution.py:232
  728.5 12.6 %pick.7.x_hbm = bf16[4,4,128,2048]{3,2,1,0:T(8,128)(2,1)S(1)} custom-call(s32[2]{0:T(128)S(1)} %get-tuple-element.55.h_ref, s32[16,4,1024]{2,1,0:T(4,128)S(1)} %broadcast_select_fusion.rank_ref, bf16[16,1024,2048]{2,1,0:T(8,128)(2,1)} %bitcast.12.u_ref), custom_call_target="tpu_custom_call" | custom-call | flops 1024 | bytes 25165824 | tf_op jit(solution)/shard_map/pick/pallas_call | solution.py:152
  744.4 55.9 %expert.9 = bf16[32768,128]{1,0:T(8,128)(2,1)} custom-call(s32[4]{0:T(128)} %get-tuple-element.69.n_ref, s32[16]{0:T(128)} %reshape.235.lst_ref, bf16[4,4,128,2048]{3,2,1,0:T(8,128)(2,1)} %copy-done.2, bf16[4,2048,1408]{2,1,0:T(8,128)(2,1)} %wg_hbm.9, bf16[4,2048,1408]{2,1,0:T(8,128)(2,1)} %wu_hbm.9, bf16[4,1408,2048]{2,1,0:T(8,128)(2,1)} %wd_hbm.9), custom_call_target="tpu_custom_call" | custom-call | flops 1024 | bytes 85983232 | tf_op jit(solution)/shard_map/expert/pallas_call | solution.py:232
  800.3 16.6 %part.4 = f32[16384,128]{1,0:T(8,128)} custom-call(s32[1]{0:T(128)S(6)} %max.19.k_ref, s32[6144]{0:T(1024)S(1)} %reshape_squeeze.28.idx_ref, f32[6144]{0:T(1024)S(1)} %bitcast.50, bf16[32768,128]{1,0:T(8,128)(2,1)} %bitcast.24.rest_0_, f32[16384,128]{1,0:T(8,128)} %collective-permute-done.3.rest_1_), custom_call_target="tpu_custom_call" | custom-call | flops 1024 | bytes 33554432 | tf_op jit(solution)/shard_map/part/pallas_call | solution.py:282
  839.5 54.5 %fusion.40 = f32[1024,10944]{0,1:T(8,128)} fusion(bf16[1024,2048]{1,0:T(8,128)(2,1)S(1)} %fusion.2, bf16[2048,10944]{0,1:T(8,128)(2,1)} %param.31), kind=kOutput, calls=%fused_computation.118 | convolution fusion | flops 45902462976 | bytes 93847552 | tf_op jit(solution)/shard_map/dot_general | solution.py:447
  894.0 62.1 %multiply_convert_fusion = bf16[1024,10944]{0,1:T(8,128)(2,1)} fusion(bf16[1024,2048]{1,0:T(8,128)(2,1)} %copy-done.16, bf16[2048,10944]{0,1:T(8,128)(2,1)} %param.32, f32[1024,10944]{0,1:T(8,128)} %fusion.40), kind=kOutput, calls=%fused_computation | convolution fusion | flops 45969702912 | bytes 116260864 | tf_op jit(solution)/shard_map/dot_general | solution.py:448
  967.1 21.5 %collective-permute-done.4.rest_1_ = f32[16384,128]{1,0:T(8,128)} collective-permute-done((f32[16384,128]{1,0:T(8,128)}, f32[16384,128]{1,0:T(8,128)}, u32[]{:S(2)}, u32[]{:S(2)}) %collective-permute-start.4) | collective-permute-done | bytes 8388640 | tf_op jit(solution)/shard_map/ppermute | solution.py:372
  988.6 15.4 %part.5 = f32[16384,128]{1,0:T(8,128)} custom-call(s32[1]{0:T(128)S(6)} %max.21.k_ref, s32[6144]{0:T(1024)S(1)} %reshape_squeeze.30.idx_ref, f32[6144]{0:T(1024)S(1)} %bitcast.49, bf16[32768,128]{1,0:T(8,128)(2,1)} %bitcast.27.rest_0_, f32[16384,128]{1,0:T(8,128)} %collective-permute-done.4.rest_1_), custom_call_target="tpu_custom_call" | custom-call | flops 1024 | bytes 33554432 | tf_op jit(solution)/shard_map/part/pallas_call | solution.py:282
  1019.6 58.9 %convolution_convert_fusion.f_ref = bf16[1024,2048]{1,0:T(8,128)(2,1)} fusion(bf16[1024,10944]{0,1:T(8,128)(2,1)} %multiply_convert_fusion, bf16[10944,2048]{1,0:T(8,128)(2,1)} %param.33), kind=kOutput, calls=%fused_computation.11 | convolution fusion | flops 45904560128 | bytes 71434240 | tf_op jit(solution)/shard_map/dot_general | solution.py:453
  1078.5 28.7 %all-to-all-done.4 = bf16[4,8192,128]{2,1,0:T(8,128)(2,1)} async-done(((bf16[4,8192,128]{2,1,0:T(8,128)(2,1)}), bf16[4,8192,128]{2,1,0:T(8,128)(2,1)}, u32[]{:S(2)}, u32[]{:S(2)}) %all-to-all-start.4) | async-done | bytes 8388640 | tf_op jit(solution)/shard_map/all_to_all | solution.py:424
  1107.2 39.6 %collective-permute-done.6.rest_1_ = f32[16384,128]{1,0:T(8,128)} collective-permute-done((f32[16384,128]{1,0:T(8,128)}, f32[16384,128]{1,0:T(8,128)}, u32[]{:S(2)}, u32[]{:S(2)}) %collective-permute-start.6) | collective-permute-done | bytes 8388640 | tf_op jit(solution)/shard_map/ppermute | solution.py:372
  1146.9 36.2 %collective-permute-done.8.rest_3_ = f32[16384,128]{1,0:T(8,128)} collective-permute-done((f32[16384,128]{1,0:T(8,128)}, f32[16384,128]{1,0:T(8,128)}, u32[]{:S(2)}, u32[]{:S(2)}) %collective-permute-start.8) | collective-permute-done | bytes 8388640 | tf_op jit(solution)/shard_map/ppermute | solution.py:372
  1189.6 23.3 %final.1 = bf16[1024,2048]{1,0:T(8,128)(2,1)} custom-call(s32[1]{0:T(128)S(6)} %max.18.k_ref, s32[6144]{0:T(1024)S(1)} %reshape_squeeze.24.idx_ref, f32[6144]{0:T(1024)S(1)} %bitcast.48, f32[1024,1]{1,0:T(8,128)S(1)} %copy.76.z_ref, bf16[1024,2048]{1,0:T(8,128)(2,1)S(1)} %copy-done.1, bf16[1024,2048]{1,0:T(8,128)(2,1)S(1)} %copy-done.9, ...), custom_call_target="tpu_custom_call" | custom-call | flops 1024 | bytes 58720256 | tf_op jit(solution)/shard_map/final/pallas_call | solution.py:309
  (186 shorter events, 143.0 us)
Async XLA Ops:
  6.5 398.1 %all-gather.5.cloned.1.call-start = ((), (), s32[]{:S(2)}) async-start(), calls=%async_computation.5 | async-start | bytes 71303168 | tf_op jit(solution)/shard_map/all_gather | solution.py:368
  8.6 22.9 %copy-start.25 = (s32[1,1024,6]{1,0,2:T(1,128)S(1)}, s32[1,1024,6]{1,0,2:T(1,128)}, u32[]{:S(2)}) copy-start(s32[1,1024,6]{1,0,2:T(1,128)} %param.22) | copy-start | bytes 73732
  28.5 70.4 %copy-start.5 = (bf16[1024,640]{1,0:T(8,128)(2,1)}, bf16[1024,640]{1,0:T(8,128)(2,1)S(1)}, u32[]{:S(2)}) copy-start(bf16[1024,640]{1,0:T(8,128)(2,1)S(1)} %get-tuple-element.39.k0) | copy-start | bytes 3932164
  60.0 55.5 %collective-permute-start = (bf16[1024,640]{1,0:T(8,128)(2,1)S(1)}, bf16[1024,640]{1,0:T(8,128)(2,1)}, u32[]{:S(2)}, u32[]{:S(2)}) collective-permute-start(bf16[1024,640]{1,0:T(8,128)(2,1)S(1)} %get-tuple-element.39.k0), channel_id=1, source_target_pairs={{0,2},{1,3},{4,6},{5,7},{8,10},{9,11},{12,14},{13,15},{16,18},{17,... | collective-permute-start | bytes 3932168 | tf_op jit(solution)/shard_map/ppermute | solution.py:374
  62.4 61.1 %collective-permute-start.1 = (bf16[1024,640]{1,0:T(8,128)(2,1)S(1)}, bf16[1024,640]{1,0:T(8,128)(2,1)}, u32[]{:S(2)}, u32[]{:S(2)}) collective-permute-start(bf16[1024,640]{1,0:T(8,128)(2,1)S(1)} %get-tuple-element.39.k0), channel_id=1, source_target_pairs={{0,1},{2,3},{4,5},{6,7},{8,9},{10,11},{12,13},{14,15},{16,17},{18,... | collective-permute-start | bytes 3932168 | tf_op jit(solution)/shard_map/ppermute | solution.py:375
  69.0 30.0 %copy-start.33 = (s32[4]{0:T(128)S(1)}, s32[4]{0:T(128)}, u32[]{:S(2)}) copy-start(s32[4]{0:T(128)} %constant.139.clone) | copy-start | bytes 52
  69.0 31.2 %copy-start.32 = (s32[4]{0:T(128)S(1)}, s32[4]{0:T(128)}, u32[]{:S(2)}) copy-start(s32[4]{0:T(128)} %constant.140.clone) | copy-start | bytes 52
  69.0 32.4 %copy-start.31 = (s32[4]{0:T(128)S(1)}, s32[4]{0:T(128)}, u32[]{:S(2)}) copy-start(s32[4]{0:T(128)} %constant.141.clone) | copy-start | bytes 52
  115.6 7.9 collective-permute-start.2
  441.9 15.9 %copy-start.22 = (pred[4,6,1024]{2,1,0:T(8,128)(4,1)S(1)}, pred[4,6,1024]{2,1,0:T(8,128)(4,1)}, u32[]{:S(2)}) copy-start(pred[4,6,1024]{2,1,0:T(8,128)(4,1)} %get-tuple-element.74) | copy-start | bytes 73732
  441.9 16.2 %copy-start.20 = (s32[64,1024]{1,0:T(8,128)S(1)}, s32[64,1024]{1,0:T(8,128)}, u32[]{:S(2)}) copy-start(s32[64,1024]{1,0:T(8,128)} %get-tuple-element.81) | copy-start | bytes 786436
  441.9 63.1 %all-to-all-start = ((bf16[4,4096,128]{2,1,0:T(8,128)(2,1)}), bf16[4,4096,128]{2,1,0:T(8,128)(2,1)}, u32[]{:S(2)}, u32[]{:S(2)}) async-start(bf16[4,4096,128]{2,1,0:T(8,128)(2,1)} %bitcast.55), calls=%async_computation | async-start | bytes 8388608 | tf_op jit(solution)/shard_map/all_to_all | solution.py:424
  481.8 29.2 %copy-start.21 = (f32[4,6,1024]{2,1,0:T(8,128)S(1)}, f32[4,6,1024]{2,1,0:T(8,128)}, u32[]{:S(2)}) copy-start(f32[4,6,1024]{2,1,0:T(8,128)} %get-tuple-element.73) | copy-start | bytes 294916
  481.8 31.3 %copy-start.17 = (bf16[1024,512]{1,0:T(8,128)(2,1)S(1)}, bf16[1024,512]{1,0:T(8,128)(2,1)}, u32[]{:S(2)}) copy-start(bf16[1024,512]{1,0:T(8,128)(2,1)} %attn.4) | copy-start | bytes 3145732
  481.8 31.3 %copy-start.18 = (bf16[1024,512]{1,0:T(8,128)(2,1)S(1)}, bf16[1024,512]{1,0:T(8,128)(2,1)}, u32[]{:S(2)}) copy-start(bf16[1024,512]{1,0:T(8,128)(2,1)} %attn.5) | copy-start | bytes 3145732
  505.0 53.0 %all-to-all-start.1 = ((bf16[4,4096,128]{2,1,0:T(8,128)(2,1)}), bf16[4,4096,128]{2,1,0:T(8,128)(2,1)}, u32[]{:S(2)}, u32[]{:S(2)}) async-start(bf16[4,4096,128]{2,1,0:T(8,128)(2,1)} %bitcast.56), calls=%async_computation.1 | async-start | bytes 8388608 | tf_op jit(solution)/shard_map/all_to_all | solution.py:424
  558.1 15.3 %copy-start.30 = (pred[4,4]{0,1:T(4,128)(4,1)S(1)}, pred[4,4]{0,1:T(4,128)(4,1)}, u32[]{:S(2)}) copy-start(pred[4,4]{0,1:T(4,128)(4,1)} %get-tuple-element.114) | copy-start | bytes 52
  568.7 231.5 %collective-permute-start.3 = (f32[16384,128]{1,0:T(8,128)}, f32[16384,128]{1,0:T(8,128)}, u32[]{:S(2)}, u32[]{:S(2)}) collective-permute-start(f32[16384,128]{1,0:T(8,128)} %part.3), channel_id=1, source_target_pairs={{12,8},{0,4},{13,9},{1,5},{14,10},{2,6},{15,11},{3,7},{28,24},{16,... | collective-permute-start | bytes 25165832 | tf_op jit(solution)/shard_map/ppermute | solution.py:372
  646.6 5.7 copy-start.29
  646.7 7.1 copy-start.28
  646.7 9.2 copy-start.27
  646.7 153.6 %all-to-all-start.2 = ((bf16[4,8192,128]{2,1,0:T(8,128)(2,1)}), bf16[4,8192,128]{2,1,0:T(8,128)(2,1)}, u32[]{:S(2)}, u32[]{:S(2)}) async-start(bf16[4,8192,128]{2,1,0:T(8,128)(2,1)} %bitcast.53), calls=%async_computation.2 | async-start | bytes 16777216 | tf_op jit(solution)/shard_map/all_to_all | solution.py:424
  728.5 15.9 %copy-start.24 = (s32[1,6,1024]{2,1,0:T(8,128)S(1)}, s32[1,6,1024]{2,1,0:T(8,128)}, u32[]{:S(2)}) copy-start(s32[1,6,1024]{2,1,0:T(8,128)} %get-tuple-element.86) | copy-start | bytes 73732
  816.9 139.2 %collective-permute-start.5 = (f32[16384,128]{1,0:T(8,128)}, f32[16384,128]{1,0:T(8,128)}, u32[]{:S(2)}, u32[]{:S(2)}) collective-permute-start(f32[16384,128]{1,0:T(8,128)} %part.4), channel_id=1, source_target_pairs={{8,4},{4,8},{9,5},{5,9},{10,6},{6,10},{11,7},{7,11},{24,20},{20,24... | collective-permute-start | bytes 25165832 | tf_op jit(solution)/shard_map/ppermute | solution.py:372
  820.9 167.7 %collective-permute-start.4 = (f32[16384,128]{1,0:T(8,128)}, f32[16384,128]{1,0:T(8,128)}, u32[]{:S(2)}, u32[]{:S(2)}) collective-permute-start(f32[16384,128]{1,0:T(8,128)} %part.4), channel_id=1, source_target_pairs={{12,8},{0,4},{13,9},{1,5},{14,10},{2,6},{15,11},{3,7},{28,24},{16,... | collective-permute-start | bytes 25165832 | tf_op jit(solution)/shard_map/ppermute | solution.py:372
  825.5 141.7 %all-to-all-start.3 = ((bf16[4,8192,128]{2,1,0:T(8,128)(2,1)}), bf16[4,8192,128]{2,1,0:T(8,128)(2,1)}, u32[]{:S(2)}, u32[]{:S(2)}) async-start(bf16[4,8192,128]{2,1,0:T(8,128)(2,1)} %bitcast.54), calls=%async_computation.3 | async-start | bytes 16777216 | tf_op jit(solution)/shard_map/all_to_all | solution.py:424
  965.8 181.0 %collective-permute-start.6 = (f32[16384,128]{1,0:T(8,128)}, f32[16384,128]{1,0:T(8,128)}, u32[]{:S(2)}, u32[]{:S(2)}) collective-permute-start(f32[16384,128]{1,0:T(8,128)} %add.163), channel_id=1, source_target_pairs={{4,0},{8,12},{5,1},{9,13},{6,2},{10,14},{7,3},{11,15},{20,16},{24,... | collective-permute-start | bytes 25165832 | tf_op jit(solution)/shard_map/ppermute | solution.py:372
  1004.0 142.9 %collective-permute-start.7 = (f32[16384,128]{1,0:T(8,128)}, f32[16384,128]{1,0:T(8,128)}, u32[]{:S(2)}, u32[]{:S(2)}) collective-permute-start(f32[16384,128]{1,0:T(8,128)} %part.5), channel_id=1, source_target_pairs={{4,8},{8,4},{5,9},{9,5},{6,10},{10,6},{7,11},{11,7},{20,24},{24,20... | collective-permute-start | bytes 25165832 | tf_op jit(solution)/shard_map/ppermute | solution.py:372
  1007.9 175.2 %collective-permute-start.8 = (f32[16384,128]{1,0:T(8,128)}, f32[16384,128]{1,0:T(8,128)}, u32[]{:S(2)}, u32[]{:S(2)}) collective-permute-start(f32[16384,128]{1,0:T(8,128)} %part.5), channel_id=1, source_target_pairs={{0,4},{12,8},{1,5},{13,9},{2,6},{14,10},{3,7},{15,11},{16,20},{28,... | collective-permute-start | bytes 25165832 | tf_op jit(solution)/shard_map/ppermute | solution.py:372
  1012.9 5.9 copy-start.23
  1012.9 6.5 copy-start.26
  1012.9 94.3 %all-to-all-start.4 = ((bf16[4,8192,128]{2,1,0:T(8,128)(2,1)}), bf16[4,8192,128]{2,1,0:T(8,128)(2,1)}, u32[]{:S(2)}, u32[]{:S(2)}) async-start(bf16[4,8192,128]{2,1,0:T(8,128)(2,1)} %bitcast.52), calls=%async_computation.4 | async-start | bytes 16777216 | tf_op jit(solution)/shard_map/all_to_all | solution.py:424
  (17 other events, 39.1 us)
Sparse Core Ops, SparseCore 0:
  60.2 344.4 all-gather.4
